TPU v7x, 32 devices: a whole 2x2x4 slice. The times are simulated.
32 devices in a mesh: gx: 4 (over x, core), gy: 8 (over z, y).
Axes of the slice: x: 2, y: 2, z: 4, core: 2. Of those that a mesh axis runs over, the one named last changes fastest.
Arguments:
- electric: float32 [3, 64, 128, 256], P(None, 'gx', 'gy'), may hold values from -6 to 6
- magnetic: float32 [3, 64, 128, 256], P(None, 'gx', 'gy'), may hold values from -6 to 6
- aux_electric: float32 [6, 64, 128, 256], P(None, 'gx', 'gy'), may hold values from -3 to 3
- aux_magnetic: float32 [6, 64, 128, 256], P(None, 'gx', 'gy'), may hold values from -3 to 3
- grades: int32 [3, 64, 128, 256], P(None, 'gx', 'gy'), may hold values from 0 to 3
- permittivity: float32 [64, 128, 256], P('gx', 'gy'), may hold values from 1 to 8
- dipole_cell: int32 [3, 16384], P(None, ('gx', 'gy')), may hold values from 0 to 255, as said below
- dipole_port: int32 [16384], P(('gx', 'gy')), may hold values from 0 to 511
- live_count: int32 [32], P(('gx', 'gy')), may hold values from 1 to 512, as said below
- injection: bfloat16 [16384, 512], P(('gx', 'gy')), may hold values from -0.25 to 0.25
- waveform: bfloat16 [512, 16], replicated, may hold values from -6 to 6
Outputs:
- electric_out: float32 [3, 64, 128, 256], P(None, 'gx', 'gy')
- magnetic_out: float32 [3, 64, 128, 256], P(None, 'gx', 'gy')
- port_power: float32 [16, 512], replicated
Inputs may be any that keep to these rules, and one draw needn't show every extreme that they name: `dipole_cell`: slot s lies in the block of cells held by the device that holds slot s. The live slots of a device are its first live_count ones; some device has all 512 live.
All inputs are finite; a program needn't handle non-finite values.
Results may differ from a plain program's by a relative error of at most 0.0003.
Values sent between devices are 32-bit elements; how exact they have to be, the bound alone decides.
A program may use at most 128 MiB of HBM per device.

v0:
```python
import functools

import jax
import jax.numpy as jnp
from jax import lax
from jax.experimental import pallas as pl
from jax.experimental.pallas import tpu as pltpu
from jax.sharding import PartitionSpec as P

MESH = pl.DeviceIdType.MESH
courant = 0.55
absorb_keep = (0.0, 0.92, 0.75, 0.45)
absorb_take = (0.0, -0.06, -0.18, -0.35)
derivative_pairs = ((2, 1), (1, 2), (0, 2), (2, 0), (1, 0), (0, 1))
UNROLL = 4


def grade_table(grades, table):
    result = jnp.where(grades == 1, table[1], 0.0)
    result = jnp.where(grades == 2, table[2], result)
    return jnp.where(grades == 3, table[3], result)


def split_two(values):
    high = values.astype(jnp.bfloat16)
    low = (values - high.astype(jnp.float32)).astype(jnp.bfloat16)
    return high, low


def kernel(
    e_in, h_in, me_in, mh_in, grades_ref, eps_ref, cell_ref, port_ref, live_ref, inj_ref, wave_ref,
    e_out, h_out, power_ref,
    ef, hf, me, mh, keep, take, factor, source,
    send_e, recv_e, send_h, recv_h, cell_t, cell_f, depth_t, depth, current, record,
    share, from_y, from_x, result,
    load_sem, store_sem, send_sem, recv_sem, send_sum, recv_sum,
):
    depth_x, depth_y, depth_z = eps_ref.shape
    ports, slots = inj_ref.shape[1], inj_ref.shape[0]
    steps = wave_ref.shape[0]
    ix, iy = lax.axis_index("gx"), lax.axis_index("gy")
    count_x, count_y = lax.axis_size("gx"), lax.axis_size("gy")
    has_left, has_right = ix > 0, ix < count_x - 1
    has_down, has_up = iy > 0, iy < count_y - 1

    loads = [
        pltpu.make_async_copy(e_in, ef.at[:, pl.ds(0, depth_x)], load_sem.at[0]),
        pltpu.make_async_copy(h_in, hf.at[:, pl.ds(1, depth_x)], load_sem.at[1]),
        pltpu.make_async_copy(me_in, me, load_sem.at[2]),
        pltpu.make_async_copy(mh_in, mh, load_sem.at[3]),
    ]
    for copy in loads:
        copy.start()

    plane = jnp.zeros((depth_y, depth_z), jnp.float32)
    for component in (1, 2):
        ef[component, depth_x] = plane
        hf[component, 0] = plane
    recv_e[...] = jnp.zeros(recv_e.shape, jnp.float32)
    recv_h[...] = jnp.zeros(recv_h.shape, jnp.float32)

    barrier = pltpu.get_barrier_semaphore()
    line_x = [(lax.rem(ix + offset, count_x), iy) for offset in range(1, count_x)]
    line_y = [(ix, lax.rem(iy + offset, count_y)) for offset in range(1, count_y)]
    for peer in line_x + line_y:
        pl.semaphore_signal(barrier, inc=1, device_id=peer, device_id_type=MESH)

    cells = (cell_ref[0:1, :] - ix * depth_x) * depth_y + (cell_ref[1:2, :] - iy * depth_y)
    hit = lax.broadcasted_iota(jnp.int32, cell_f.shape, 0) == cells
    cell_f[...] = jnp.where(hit, 1.0, 0.0)
    cell_t[...] = jnp.where(hit, 1.0, 0.0).astype(jnp.bfloat16)
    hit = lax.broadcasted_iota(jnp.int32, depth_t.shape, 0) == cell_ref[2:3, :]
    table = jnp.where(hit, 1.0, 0.0)
    depth_t[...] = table.astype(jnp.bfloat16)
    depth[...] = table.T.astype(jnp.bfloat16)
    live = lax.broadcasted_iota(jnp.int32, (1, slots), 1) < live_ref[0]
    flow = lax.dot_general(
        wave_ref[...], inj_ref[...], (((1,), (1,)), ((), ())), preferred_element_type=jnp.float32
    )
    current[...] = jnp.where(live, flow, 0.0)

    def prepare(x, _):
        for d in range(3):
            level = grades_ref[d, x]
            keep[d, x] = grade_table(level, absorb_keep)
            take[d, x] = grade_table(level, absorb_take)
        factor[x] = courant / eps_ref[x]
        return 0

    lax.fori_loop(0, depth_x, prepare, 0)
    for copy in loads:
        copy.wait()

    def pack_first(x):
        send_e[0, pl.ds(x, 1), :] = ef[0, x, 0:1, :]
        send_e[1, pl.ds(x, 1), :] = ef[2, x, 0:1, :]

    for x in range(depth_x):
        pack_first(x)
    pl.semaphore_wait(barrier, len(line_x) + len(line_y))

    def copies(kind):
        if kind == 0:
            return (
                (has_left, has_right, pltpu.make_async_remote_copy(
                    src_ref=ef.at[pl.ds(1, 2), 0], dst_ref=ef.at[pl.ds(1, 2), depth_x],
                    send_sem=send_sem.at[0], recv_sem=recv_sem.at[0],
                    device_id=(ix - 1, iy), device_id_type=MESH)),
                (has_down, has_up, pltpu.make_async_remote_copy(
                    src_ref=send_e, dst_ref=recv_e,
                    send_sem=send_sem.at[1], recv_sem=recv_sem.at[1],
                    device_id=(ix, iy - 1), device_id_type=MESH)),
            )
        return (
            (has_right, has_left, pltpu.make_async_remote_copy(
                src_ref=hf.at[pl.ds(1, 2), depth_x], dst_ref=hf.at[pl.ds(1, 2), 0],
                send_sem=send_sem.at[2], recv_sem=recv_sem.at[2],
                device_id=(ix + 1, iy), device_id_type=MESH)),
            (has_up, has_down, pltpu.make_async_remote_copy(
                src_ref=send_h, dst_ref=recv_h,
                send_sem=send_sem.at[3], recv_sem=recv_sem.at[3],
                device_id=(ix, iy + 1), device_id_type=MESH)),
        )

    def start(kind, side, wanted=True):
        sends, _, copy = copies(kind)[side]
        pl.when(jnp.logical_and(sends, wanted))(copy.start)

    def finish(kind):
        for sends, receives, copy in copies(kind):
            pl.when(sends)(copy.wait_send)
            pl.when(receives)(copy.wait_recv)

    rows = lax.broadcasted_iota(jnp.int32, (depth_y, depth_z), 0)
    lanes = lax.broadcasted_iota(jnp.int32, (depth_y, depth_z), 1)

    def curl(x, here, beside, halo, memory, forward):
        turn_y = depth_y - 1 if forward else 1
        turn_z = depth_z - 1 if forward else 1
        edge_y = rows == (depth_y - 1 if forward else 0)
        edge_z = lanes == (depth_z - 1 if forward else 0)
        terms = []
        for number, (component, axis) in enumerate(derivative_pairs):
            value = here[component]
            if axis == 0:
                other = beside[component]
            elif axis == 1:
                line = halo[component // 2, pl.ds(x, 1), :]
                other = jnp.where(edge_y, line, pltpu.roll(value, turn_y, 0))
            else:
                other = jnp.where(edge_z, 0.0, pltpu.roll(value, turn_z, 1))
            slope = other - value if forward else value - other
            carried = keep[axis, x] * memory[number, x] + take[axis, x] * slope
            memory[number, x] = carried
            terms.append(slope + carried)
        return (terms[0] - terms[1], terms[2] - terms[3], terms[4] - terms[5])

    def update_h(block, _):
        for inner in range(UNROLL):
            x = block * UNROLL + inner
            here = [ef[c, x] for c in range(3)]
            beside = [None, ef[1, x + 1], ef[2, x + 1]]
            rotation = curl(x, here, beside, recv_e, me, True)
            fresh = [hf[c, x + 1] - courant * rotation[c] for c in range(3)]
            for c in range(3):
                hf[c, x + 1] = fresh[c]
            send_h[0, pl.ds(x, 1), :] = fresh[0][depth_y - 1:depth_y, :]
            send_h[1, pl.ds(x, 1), :] = fresh[2][depth_y - 1:depth_y, :]
        return 0

    def update_e(block, _):
        for inner in range(UNROLL):
            x = block * UNROLL + inner
            here = [hf[c, x + 1] for c in range(3)]
            beside = [None, hf[1, x], hf[2, x]]
            rotation = curl(x, here, beside, recv_h, mh, False)
            ratio = factor[x]
            fresh = [ef[c, x] + ratio * rotation[c] for c in range(3)]
            fresh[2] = fresh[2] - courant * source[x]
            for c in range(3):
                ef[c, x] = fresh[c]
            send_e[0, pl.ds(x, 1), :] = fresh[0][0:1, :]
            send_e[1, pl.ds(x, 1), :] = fresh[2][0:1, :]
        return 0

    def inject(step):
        high, low = split_two(current[pl.ds(step, 1), :])
        total = None
        for part in (high, low):
            piece = jnp.dot(
                cell_t[...] * part, depth[...], preferred_element_type=jnp.float32
            )
            total = piece if total is None else total + piece
        source[...] = total.reshape(source.shape)

    def read_out(step):
        values = ef[2, pl.ds(0, depth_x)].reshape(depth_x * depth_y, depth_z)
        high, low = split_two(values)
        picked = jnp.dot(high, depth_t[...], preferred_element_type=jnp.float32)
        picked = picked + jnp.dot(low, depth_t[...], preferred_element_type=jnp.float32)
        chosen = jnp.sum(picked * cell_f[...], axis=0, keepdims=True)
        record[pl.ds(step, 1), :] = chosen * current[pl.ds(step, 1), :]

    blocks = depth_x // UNROLL

    def turn(step, _):
        inject(step)
        finish(0)
        update_h(blocks - 1, 0)
        start(1, 0)
        lax.fori_loop(0, blocks - 1, update_h, 0)
        start(1, 1)
        read_out((step + steps - 1) % steps)
        finish(1)
        more = step < steps - 1
        update_e(0, 0)
        start(0, 0, more)
        lax.fori_loop(1, blocks, update_e, 0)
        start(0, 1, more)
        return 0

    start(0, 1)
    start(0, 0)
    lax.fori_loop(0, steps, turn, 0)
    stores = [
        pltpu.make_async_copy(ef.at[:, pl.ds(0, depth_x)], e_out, store_sem.at[0]),
        pltpu.make_async_copy(hf.at[:, pl.ds(1, depth_x)], h_out, store_sem.at[1]),
    ]
    for copy in stores:
        copy.start()
    read_out(steps - 1)
    member = lax.broadcasted_iota(jnp.int32, (ports, slots), 0) == port_ref[...]
    member = jnp.where(member, 1.0, 0.0).astype(jnp.bfloat16)
    total = None
    for part in split_two(record[...]):
        piece = lax.dot_general(
            part, member, (((1,), (1,)), ((), ())), preferred_element_type=jnp.float32
        )
        total = piece if total is None else total + piece
    for row in range(steps):
        share[row] = total[row:row + 1, :]
    chunk = steps // count_y

    def spread(first, peers, source_of, target):
        moves = []
        for number, peer in enumerate(peers):
            moves.append(pltpu.make_async_remote_copy(
                src_ref=source_of(peer), dst_ref=target,
                send_sem=send_sum.at[first + number], recv_sem=recv_sum.at[first + number],
                device_id=peer, device_id_type=MESH))
            moves[-1].start()
        return moves

    def settle(moves):
        for move in moves:
            move.wait()

    mine = pl.ds(iy * chunk, chunk)
    moves = spread(
        0, line_y, lambda peer: share.at[pl.ds(peer[1] * chunk, chunk)], from_y.at[iy]
    )
    from_y[iy] = share[mine]
    settle(moves)
    from_x[ix] = sum(from_y[j] for j in range(count_y))
    first = len(line_y)
    settle(spread(first, line_x, lambda peer: from_x.at[ix], from_x.at[ix]))
    result[mine] = sum(from_x[i] for i in range(count_x))
    first = first + len(line_x)
    settle(spread(first, line_y, lambda peer: result.at[mine], result.at[mine]))
    for row in range(steps):
        power_ref[row:row + 1, :] = result[row]
    for copy in stores:
        copy.wait()


def local(
    electric, magnetic, aux_electric, aux_magnetic, grades, permittivity,
    dipole_cell, dipole_port, live_count, injection, waveform,
):
    depth_x, depth_y, depth_z = permittivity.shape
    slots = dipole_cell.shape[1]
    ports, steps = waveform.shape
    block = (depth_x, depth_y, depth_z)
    cells = depth_x * depth_y
    f32 = jnp.float32
    count_x, count_y = lax.axis_size("gx"), lax.axis_size("gy")
    chunk = steps // count_y
    assert chunk * count_y == steps
    transfers = count_x + 2 * count_y
    vmem = pl.BlockSpec(memory_space=pltpu.VMEM)
    anywhere = pl.BlockSpec(memory_space=pltpu.HBM)
    electric, magnetic, power = pl.pallas_call(
        kernel,
        out_shape=(
            jax.ShapeDtypeStruct(electric.shape, f32),
            jax.ShapeDtypeStruct(magnetic.shape, f32),
            jax.ShapeDtypeStruct((steps, ports), f32),
        ),
        in_specs=[anywhere] * 4 + [vmem] * 4
        + [pl.BlockSpec(memory_space=pltpu.SMEM)] + [vmem] * 2,
        out_specs=(anywhere, anywhere, vmem),
        scratch_shapes=[
            pltpu.VMEM((3, depth_x + 1, depth_y, depth_z), f32),
            pltpu.VMEM((3, depth_x + 1, depth_y, depth_z), f32),
            pltpu.VMEM((6,) + block, f32),
            pltpu.VMEM((6,) + block, f32),
            pltpu.VMEM((3,) + block, f32),
            pltpu.VMEM((3,) + block, f32),
            pltpu.VMEM(block, f32),
            pltpu.VMEM(block, f32),
            pltpu.VMEM((2, depth_x, depth_z), f32),
            pltpu.VMEM((2, depth_x, depth_z), f32),
            pltpu.VMEM((2, depth_x, depth_z), f32),
            pltpu.VMEM((2, depth_x, depth_z), f32),
            pltpu.VMEM((cells, slots), jnp.bfloat16),
            pltpu.VMEM((cells, slots), f32),
            pltpu.VMEM((depth_z, slots), jnp.bfloat16),
            pltpu.VMEM((slots, depth_z), jnp.bfloat16),
            pltpu.VMEM((steps, slots), f32),
            pltpu.VMEM((steps, slots), f32),
            pltpu.VMEM((steps, 1, ports), f32),
            pltpu.VMEM((count_y, chunk, 1, ports), f32),
            pltpu.VMEM((count_x, chunk, 1, ports), f32),
            pltpu.VMEM((steps, 1, ports), f32),
            pltpu.SemaphoreType.DMA((4,)),
            pltpu.SemaphoreType.DMA((2,)),
            pltpu.SemaphoreType.DMA((4,)),
            pltpu.SemaphoreType.DMA((4,)),
            pltpu.SemaphoreType.DMA((transfers,)),
            pltpu.SemaphoreType.DMA((transfers,)),
        ],
        compiler_params=pltpu.CompilerParams(
            collective_id=0, has_side_effects=True, vmem_limit_bytes=60 * 1024 * 1024
        ),
    )(
        electric, magnetic, aux_electric, aux_magnetic, grades, permittivity,
        dipole_cell, dipole_port.reshape(1, slots), live_count, injection, waveform.T,
    )
    return electric, magnetic, power


def solution(mesh):
    in_specs = (
        P(None, "gx", "gy", None),
        P(None, "gx", "gy", None),
        P(None, "gx", "gy", None),
        P(None, "gx", "gy", None),
        P(None, "gx", "gy", None),
        P("gx", "gy", None),
        P(None, ("gx", "gy")),
        P(("gx", "gy")),
        P(("gx", "gy")),
        P(("gx", "gy"), None),
        P(),
    )
    out_specs = (P(None, "gx", "gy", None), P(None, "gx", "gy", None), P())
    return jax.shard_map(local, mesh=mesh, in_specs=in_specs, out_specs=out_specs, check_vma=False)
```

profile of v0, /device:TPU:0, one launch (start us, length us, event | category | flops | bytes accessed | tf_op | source)
XLA Modules:
  0.0 147.8 jit_solution(13856747401808787073)
XLA Ops:
  1.3 142.9 %shard_map.130 = (f32[3,16,16,256]{3,2,1,0:T(8,128)}, f32[3,16,16,256]{3,2,1,0:T(8,128)}, f32[16,512]{1,0:T(8,128)}) custom-call(f32[3,16,16,256]{3,2,1,0:T(8,128)} %e_in.1, f32[3,16,16,256]{3,2,1,0:T(8,128)} %h_in.1, f32[6,16,16,256]{3,2,1,0:T(8,128)} %me_in.1, f32[6,16,16,256]{3,2,1,0:T(8,128)} %mh_in.1, s32[3,16,16,256]{3,2,1,0:T(8,128)} %grades_ref.1, ...), custom_call_target="tpu_custom_call" | custom-call | tf_op jit(solution)/shard_map/pallas_call | solution.py:292
  144.2 0.0 copy-start
  144.2 0.0 copy-start.1
  144.2 2.1 %copy.18 = f32[3,16,16,256]{3,2,1,0:T(8,128)} copy(f32[3,16,16,256]{3,2,1,0:T(8,128)} %get-tuple-element.6) | data formatting | bytes 1572864
  146.3 0.0 copy-done
  146.3 0.9 copy.19
  147.2 0.0 copy-done.1
  147.2 0.6 copy.20
Async XLA Ops:
  144.2 2.2 %copy-start = (f32[3,16,16,256]{3,2,1,0:T(8,128)S(1)}, f32[3,16,16,256]{3,2,1,0:T(8,128)}, u32[]{:S(2)}) copy-start(f32[3,16,16,256]{3,2,1,0:T(8,128)} %get-tuple-element.7) | copy-start | bytes 2359300
  144.2 3.0 %copy-start.1 = (f32[16,512]{1,0:T(8,128)S(1)}, f32[16,512]{1,0:T(8,128)}, u32[]{:S(2)}) copy-start(f32[16,512]{1,0:T(8,128)} %get-tuple-element.8) | copy-start | bytes 98308
where the time goes:
time: 148 us
  Pallas kernels  143 us (97%)
  local copies, waits for them, and re-layouts  3.64 us (2%)
    pallas_call x1, Pallas kernels, local(): pl.pallas_call(kernel, out_shape=(jax.ShapeDtypeStruct(electric.shape, f3...  143 us
    unnamed x7, local copies, waits for them, and re-layouts  3.64 us

commit v1 on v0

v1 whole, which is shorter than its diff:
```python
import functools

import jax
import jax.numpy as jnp
from jax import lax
from jax.experimental import pallas as pl
from jax.experimental.pallas import tpu as pltpu
from jax.sharding import PartitionSpec as P

MESH = pl.DeviceIdType.MESH
courant = 0.55
absorb_keep = (0.0, 0.92, 0.75, 0.45)
absorb_take = (0.0, -0.06, -0.18, -0.35)
derivative_pairs = ((2, 1), (1, 2), (0, 2), (2, 0), (1, 0), (0, 1))
UNROLL = 4


def grade_table(grades, table):
    result = jnp.where(grades == 1, table[1], 0.0)
    result = jnp.where(grades == 2, table[2], result)
    return jnp.where(grades == 3, table[3], result)


def split_two(values):
    high = values.astype(jnp.bfloat16)
    low = (values - high.astype(jnp.float32)).astype(jnp.bfloat16)
    return high, low


KINDS = ("ay", "by", "axh", "axl", "bxl", "bxh", "d1", "d2")
TRAVEL = {
    "ay": (0, 1), "by": (0, -1), "axh": (1, 0), "axl": (1, 0),
    "bxl": (-1, 0), "bxh": (-1, 0), "d1": (-1, 1), "d2": (1, -1),
}
COEFFICIENTS = ((0, 1), (0, -1), (1, 0), (-1, 0), (-1, 1), (1, -1))
SLOTS = 4


def kernel(
    e_in, h_in, me_in, mh_in, grades_ref, eps_ref, cell_ref, port_ref, live_ref, inj_ref, wave_ref,
    e_out, h_out, power_ref,
    ef, hf, me, mh, keep, take, factor, source,
    say, sby, saxh, saxl, sbxl, sbxh, sd1, sd2,
    ray, rby, raxh, raxl, rbxl, rbxh, rd1, rd2,
    cs_up, cs_down, cs_right, cs_left, cs_d1, cs_d2,
    cr_up, cr_down, cr_right, cr_left, cr_d1, cr_d2,
    row_h, row_e, save_row_h, save_row_e, save_h_lo, save_h_hi, save_e_lo, save_e_hi, lines,
    edge_h, edge_ht, edge_e, edge_et,
    cell_t, cell_f, depth_t, depth, current, record, z_copy,
    share, from_y, from_x, result,
    load_sem, store_sem, send_sem, recv_sem, send_one, recv_one, send_sum, recv_sum,
):
    depth_x, depth_y, depth_z = eps_ref.shape
    ports, slots = inj_ref.shape[1], inj_ref.shape[0]
    steps = wave_ref.shape[0]
    half = depth_y // 2
    last_x, last_y = depth_x - 1, depth_y - 1
    ix, iy = lax.axis_index("gx"), lax.axis_index("gy")
    count_x, count_y = lax.axis_size("gx"), lax.axis_size("gy")
    f32 = jnp.float32

    def there(dx, dy):
        found = ix >= 0
        if dx:
            found = jnp.logical_and(found, ix > 0 if dx < 0 else ix < count_x - 1)
        if dy:
            found = jnp.logical_and(found, iy > 0 if dy < 0 else iy < count_y - 1)
        return found

    loads = [
        pltpu.make_async_copy(e_in, ef.at[:, pl.ds(0, depth_x)], load_sem.at[0]),
        pltpu.make_async_copy(h_in, hf.at[:, pl.ds(1, depth_x)], load_sem.at[1]),
        pltpu.make_async_copy(me_in, me, load_sem.at[2]),
        pltpu.make_async_copy(mh_in, mh, load_sem.at[3]),
    ]
    for copy in loads:
        copy.start()

    plane = jnp.zeros((depth_y, depth_z), f32)
    for component in range(3):
        ef[component, depth_x] = plane
        hf[component, 0] = plane
    for ref in (
        ray, rby, raxh, raxl, rbxl, rbxh, rd1, rd2,
        cr_up, cr_down, cr_right, cr_left, cr_d1, cr_d2,
        save_row_h, save_h_lo, save_h_hi, lines, sd2, cs_up, cs_down, cs_right, cs_left, cs_d1, cs_d2,
    ):
        ref[...] = jnp.zeros(ref.shape, f32)

    barrier = pltpu.get_barrier_semaphore()
    line_x = [(lax.rem(ix + offset, count_x), iy) for offset in range(1, count_x)]
    line_y = [(ix, lax.rem(iy + offset, count_y)) for offset in range(1, count_y)]
    across = [
        (lax.rem(ix + count_x - 1, count_x), lax.rem(iy + 1, count_y)),
        (lax.rem(ix + 1, count_x), lax.rem(iy + count_y - 1, count_y)),
    ]
    for peer in line_x + line_y + across:
        pl.semaphore_signal(barrier, inc=1, device_id=peer, device_id_type=MESH)

    def prepare(x, _):
        for d in range(3):
            level = grades_ref[d, x]
            keep[d, x] = grade_table(level, absorb_keep)
            take[d, x] = grade_table(level, absorb_take)
        factor[x] = courant / eps_ref[x]
        return 0

    lax.fori_loop(0, depth_x, prepare, 0)

    row_half = lax.broadcasted_iota(jnp.int32, (half, depth_z), 0)
    is_top, is_bottom = row_half == half - 1, row_half == 0

    for x in range(depth_x):
        upper = take[1, x, half:, :]
        lower = take[1, x, :half, :]
        scale_h = courant * (1.0 + upper)
        scale_e = factor[x, :half, :] * (1.0 + lower)
        edge_h[x] = jnp.where(is_top, scale_h, 0.0)
        edge_ht[x] = jnp.where(is_top, upper, 0.0)
        edge_e[x] = jnp.where(is_bottom, scale_e, 0.0)
        edge_et[x] = jnp.where(is_bottom, lower, 0.0)
        cs_up[x:x + 1, :] = scale_h[half - 1:half, :]
        cs_down[x:x + 1, :] = scale_e[0:1, :]
    cs_right[0:depth_y, :] = courant * (1.0 + take[0, last_x])
    cs_left[0:depth_y, :] = factor[0] * (1.0 + take[0, 0])
    cs_up[depth_x:depth_x + 1, :] = cs_right[last_y:depth_y, :]
    cs_down[depth_x:depth_x + 1, :] = cs_left[0:1, :]
    cs_right[depth_y:depth_y + 1, :] = cs_up[last_x:depth_x, :]
    cs_left[depth_y:depth_y + 1, :] = cs_down[0:1, :]
    cs_d1[0:1, :] = cs_up[0:1, :]
    cs_d2[0:1, :] = cs_down[last_x:depth_x, :]

    once = []
    for number, (source_ref, target_ref) in enumerate((
        (cs_up, cr_up), (cs_down, cr_down), (cs_right, cr_right),
        (cs_left, cr_left), (cs_d1, cr_d1), (cs_d2, cr_d2),
    )):
        dx, dy = COEFFICIENTS[number]
        once.append((there(dx, dy), there(-dx, -dy), pltpu.make_async_remote_copy(
            src_ref=source_ref, dst_ref=target_ref,
            send_sem=send_one.at[number], recv_sem=recv_one.at[number],
            device_id=(ix + dx, iy + dy), device_id_type=MESH)))

    sends = dict(ay=say, by=sby, axh=saxh, axl=saxl, bxl=sbxl, bxh=sbxh, d1=sd1, d2=sd2)
    gets = dict(ay=ray, by=rby, axh=raxh, axl=raxl, bxl=rbxl, bxh=rbxh, d1=rd1, d2=rd2)

    def message(kind, step):
        number = KINDS.index(kind)
        slot = lax.rem(step, SLOTS)
        dx, dy = TRAVEL[kind]
        return pltpu.make_async_remote_copy(
            src_ref=sends[kind], dst_ref=gets[kind].at[slot],
            send_sem=send_sem.at[number], recv_sem=recv_sem.at[number, slot],
            device_id=(ix + dx, iy + dy), device_id_type=MESH)

    def send(step, *kinds):
        for kind in kinds:
            dx, dy = TRAVEL[kind]
            pl.when(there(dx, dy))(message(kind, step).start)

    def sent(step, *kinds):
        for kind in kinds:
            dx, dy = TRAVEL[kind]
            pl.when(there(dx, dy))(message(kind, step).wait_send)

    def arrived(step, *kinds):
        for kind in kinds:
            dx, dy = TRAVEL[kind]
            pl.when(there(-dx, -dy))(message(kind, step).wait_recv)

    low, high = slice(0, half), slice(half, depth_y)
    lanes = lax.broadcasted_iota(jnp.int32, (half, depth_z), 1)
    z_last, z_first = lanes == depth_z - 1, lanes == 0

    def curl(x, part, here, beside, line, memory, forward):
        turn_y = half - 1 if forward else 1
        turn_z = depth_z - 1 if forward else 1
        edge_y = is_top if forward else is_bottom
        edge_z = z_last if forward else z_first
        terms = []
        for number, (component, axis) in enumerate(derivative_pairs):
            value = here[component]
            if axis == 0:
                other = beside[component]
            elif axis == 1:
                other = jnp.where(edge_y, line[component], pltpu.roll(value, turn_y, 0))
            else:
                other = jnp.where(edge_z, 0.0, pltpu.roll(value, turn_z, 1))
            slope = other - value if forward else value - other
            carried = keep[axis, x, part] * memory[number, x, part] + take[axis, x, part] * slope
            memory[number, x, part] = carried
            terms.append(slope + carried)
        return (terms[0] - terms[1], terms[2] - terms[3], terms[4] - terms[5])

    blocks = depth_x // UNROLL
    no_line = [0.0, None, 0.0]

    def update_h(upper):
        part = high if upper else low

        def run(block, _):
            for inner in range(UNROLL):
                x = block * UNROLL + inner
                here = [ef[c, x, part] for c in range(3)]
                beside = [None, ef[1, x + 1, part], ef[2, x + 1, part]]
                line = no_line
                if not upper:
                    line = [ef[0, x, half:half + 1, :], None, ef[2, x, half:half + 1, :]]
                rotation = curl(x, part, here, beside, line, me, True)
                fresh = [hf[c, x + 1, part] - courant * rotation[c] for c in range(3)]
                for c in range(3):
                    hf[c, x + 1, part] = fresh[c]
                z_copy[x, part] = here[2]
                if upper:
                    say[0, pl.ds(x, 1), :] = fresh[0][half - 1:half, :]
                    say[1, pl.ds(x, 1), :] = fresh[2][half - 1:half, :]
            return 0

        lax.fori_loop(0, blocks, run, 0)

    def update_e(upper):
        part = high if upper else low

        def run(block, _):
            for inner in range(UNROLL):
                x = block * UNROLL + inner
                here = [hf[c, x + 1, part] for c in range(3)]
                beside = [None, hf[1, x, part], hf[2, x, part]]
                line = no_line
                if upper:
                    line = [hf[0, x + 1, half - 1:half, :], None, hf[2, x + 1, half - 1:half, :]]
                rotation = curl(x, part, here, beside, line, mh, False)
                ratio = factor[x, part]
                fresh = [ef[c, x, part] + ratio * rotation[c] for c in range(3)]
                fresh[2] = fresh[2] - source[x, part]
                for c in range(3):
                    ef[c, x, part] = fresh[c]
                if not upper:
                    sby[0, pl.ds(x, 1), :] = fresh[0][0:1, :]
                    sby[1, pl.ds(x, 1), :] = fresh[2][0:1, :]
            return 0

        lax.fori_loop(0, blocks, run, 0)

    def fix_h_side(part, side_y, side_z):
        scale = cs_right[part]
        amount = take[0, last_x, part]
        hf[1, depth_x, part] = hf[1, depth_x, part] + scale * side_z
        hf[2, depth_x, part] = hf[2, depth_x, part] - scale * side_y
        me[3, last_x, part] = me[3, last_x, part] + amount * side_z
        me[4, last_x, part] = me[4, last_x, part] + amount * side_y

    def fix_e_side(part, side_y, side_z):
        scale = cs_left[part]
        amount = take[0, 0, part]
        ef[1, 0, part] = ef[1, 0, part] + scale * side_z
        ef[2, 0, part] = ef[2, 0, part] - scale * side_y
        mh[3, 0, part] = mh[3, 0, part] - amount * side_z
        mh[4, 0, part] = mh[4, 0, part] - amount * side_y

    ey_corner, hx_corner, ez_edge, ex_corner, hz_edge = (pl.ds(8 * n, 1) for n in range(5))
    rows_x, rows_y = pl.ds(0, depth_x), pl.ds(0, depth_y)

    def settle_e_low(step):
        arrived(step, "ay", "d1", "axl")
        slot = lax.rem(step, SLOTS)
        scale = cr_up[rows_x]
        below_x = ray[slot, 0] - scale * save_row_e[1]
        below_z = ray[slot, 1] + scale * save_row_e[0]
        row_h[0] = below_x
        row_h[1] = below_z
        row_h[1, last_x:depth_x, :] = (
            row_h[1, last_x:depth_x, :] - cr_up[depth_x:depth_x + 1, :] * rd1[slot, 1:2, :])
        scale = cr_right[low]
        side_y = raxl[slot, 0] + scale * save_e_lo[1]
        side_z = raxl[slot, 1] - scale * save_e_lo[0]
        lines[hx_corner] = rd1[slot, 0:1, :] - cr_d1[0:1, :] * lines[ez_edge]
        fix_e_side(low, side_y, side_z)
        for x in range(depth_x):
            line_hx, line_hz = row_h[0, x:x + 1, :], row_h[1, x:x + 1, :]
            amount, scale = edge_et[x], edge_e[x]
            ef[0, x, low] = ef[0, x, low] - scale * line_hz
            ef[2, x, low] = ef[2, x, low] + scale * line_hx
            mh[0, x, low] = mh[0, x, low] - amount * line_hz
            mh[5, x, low] = mh[5, x, low] - amount * line_hx
        scale = cs_down[rows_x]
        save_row_e[0] = sby[0] - scale * row_h[1]
        save_row_e[1] = sby[1] + scale * row_h[0]
        save_row_e[1, 0:1, :] = save_row_e[1, 0:1, :] - cs_down[depth_x:depth_x + 1, :] * side_y[0:1, :]
        save_e_lo[0] = ef[1, 0, low]
        save_e_lo[1] = ef[2, 0, low]

    def settle_h_low(step):
        arrived(step, "bxl")
        slot = lax.rem(step, SLOTS)
        scale = cr_left[low]
        side_y = rbxl[slot, 0] + scale * save_h_lo[1]
        side_z = rbxl[slot, 1] - scale * save_h_lo[0]
        corner = cr_left[depth_y:depth_y + 1, :] * lines[hx_corner]
        side_z = side_z + jnp.where(is_bottom, corner, 0.0)
        lines[ez_edge] = side_z[0:1, :]
        fix_h_side(low, side_y, side_z)
        save_h_lo[0] = hf[1, depth_x, low]
        save_h_lo[1] = hf[2, depth_x, low]
        sd2[0:1, :] = hf[1, depth_x, 0:1, :]

    def settle_h_high(step):
        arrived(step, "by", "d2", "bxh")
        slot = lax.rem(step, SLOTS)
        scale = cr_down[rows_x]
        row_e[0] = rby[slot, 0] - scale * save_row_h[1]
        row_e[1] = rby[slot, 1] + scale * save_row_h[0]
        row_e[1, 0:1, :] = row_e[1, 0:1, :] - cr_down[depth_x:depth_x + 1, :] * rd2[slot, 0:1, :]
        scale = cr_left[high]
        side_y = rbxh[slot, 0] + scale * save_h_hi[1]
        side_z = rbxh[slot, 1] - scale * save_h_hi[0]
        lines[ex_corner] = rd2[slot, 1:2, :] - cr_d2[0:1, :] * lines[hz_edge]
        fix_h_side(high, side_y, side_z)
        for x in range(depth_x):
            line_ex, line_ez = row_e[0, x:x + 1, :], row_e[1, x:x + 1, :]
            amount, scale = edge_ht[x], edge_h[x]
            hf[0, x + 1, high] = hf[0, x + 1, high] - scale * line_ez
            hf[2, x + 1, high] = hf[2, x + 1, high] + scale * line_ex
            me[0, x, high] = me[0, x, high] + amount * line_ez
            me[5, x, high] = me[5, x, high] + amount * line_ex
        scale = cs_up[rows_x]
        save_row_h[0] = say[0] - scale * row_e[1]
        save_row_h[1] = say[1] + scale * row_e[0]
        save_row_h[1, last_x:depth_x, :] = (
            save_row_h[1, last_x:depth_x, :] - cs_up[depth_x:depth_x + 1, :] * side_y[half - 1:half, :])
        save_h_hi[0] = hf[1, depth_x, high]
        save_h_hi[1] = hf[2, depth_x, high]

    def settle_e_high(step):
        arrived(step, "axh")
        slot = lax.rem(step, SLOTS)
        scale = cr_right[high]
        side_y = raxh[slot, 0] + scale * save_e_hi[1]
        side_z = raxh[slot, 1] - scale * save_e_hi[0]
        corner = cr_right[depth_y:depth_y + 1, :] * lines[ex_corner]
        side_z = side_z + jnp.where(is_top, corner, 0.0)
        lines[hz_edge] = side_z[half - 1:half, :]
        fix_e_side(high, side_y, side_z)
        save_e_hi[0] = ef[1, 0, high]
        save_e_hi[1] = ef[2, 0, high]

    def inject(step):
        top, rest = split_two(courant * current[pl.ds(step, 1), :])
        total = None
        for part in (top, rest):
            piece = jnp.dot(
                cell_t[...] * part, depth[...], preferred_element_type=jnp.float32
            )
            total = piece if total is None else total + piece
        source[...] = total.reshape(source.shape)

    def read_out(values, step):
        top, rest = split_two(values.reshape(depth_x * depth_y, depth_z))
        picked = jnp.dot(top, depth_t[...], preferred_element_type=jnp.float32)
        picked = picked + jnp.dot(rest, depth_t[...], preferred_element_type=jnp.float32)
        chosen = jnp.sum(picked * cell_f[...], axis=0, keepdims=True)
        record[pl.ds(step, 1), :] = chosen * current[pl.ds(step, 1), :]

    pl.semaphore_wait(barrier, len(line_x) + len(line_y) + len(across))
    for wanted, _, copy in once:
        pl.when(wanted)(copy.start)
    for copy in loads:
        copy.wait()

    for x in range(depth_x):
        sby[0, x:x + 1, :] = ef[0, x, 0:1, :]
        sby[1, x:x + 1, :] = ef[2, x, 0:1, :]
    for c in (1, 2):
        sbxl[c - 1] = ef[c, 0, low]
        sbxh[c - 1] = ef[c, 0, high]
    sd2[1:2, :] = ef[0, last_x, 0:1, :]
    send(0, "by", "bxl", "bxh", "d2")
    save_row_e[...] = sby[...]
    save_e_lo[...] = sbxl[...]
    save_e_hi[...] = sbxh[...]

    cells = (cell_ref[0:1, :] - ix * depth_x) * depth_y + (cell_ref[1:2, :] - iy * depth_y)
    hit = lax.broadcasted_iota(jnp.int32, cell_f.shape, 0) == cells
    cell_f[...] = jnp.where(hit, 1.0, 0.0)
    cell_t[...] = jnp.where(hit, 1.0, 0.0).astype(jnp.bfloat16)
    hit = lax.broadcasted_iota(jnp.int32, depth_t.shape, 0) == cell_ref[2:3, :]
    table = jnp.where(hit, 1.0, 0.0)
    depth_t[...] = table.astype(jnp.bfloat16)
    depth[...] = table.T.astype(jnp.bfloat16)
    live = lax.broadcasted_iota(jnp.int32, (1, slots), 1) < live_ref[0]
    flow = lax.dot_general(
        wave_ref[...], inj_ref[...], (((1,), (1,)), ((), ())), preferred_element_type=jnp.float32
    )
    current[...] = jnp.where(live, flow, 0.0)
    for wanted, expected, copy in once:
        pl.when(wanted)(copy.wait_send)
        pl.when(expected)(copy.wait_recv)

    def turn(step, _):
        more = step < steps
        update_h(True)
        for c in (1, 2):
            saxh[c - 1] = hf[c, depth_x, high]
        sd1[0:1, :] = say[0, 0:1, :]
        sd1[1:2, :] = ef[1, 0, last_y:depth_y, :]
        send(step, "d1", "ay", "axh")
        inject(step - 1)
        pl.when(step > 1)(lambda: settle_e_low(step - 1))
        update_h(False)
        for c in (1, 2):
            saxl[c - 1] = hf[c, depth_x, low]
        send(step, "axl")
        sent(step - 1, "by", "bxl", "d2")
        settle_h_low(step - 1)
        update_e(False)
        for c in (1, 2):
            sbxl[c - 1] = ef[c, 0, low]
        sd2[1:2, :] = sby[0, last_x:depth_x, :]
        pl.when(more)(lambda: send(step, "d2", "by", "bxl"))
        read_out(z_copy[...], lax.rem(step + steps - 2, steps))
        sent(step - 1, "bxh")
        settle_h_high(step - 1)
        update_e(True)
        for c in (1, 2):
            sbxh[c - 1] = ef[c, 0, high]
        pl.when(more)(lambda: send(step, "bxh"))
        sent(step, "ay", "axh", "d1", "axl")
        settle_e_high(step)
        return 0

    lax.fori_loop(1, steps + 1, turn, 0)
    settle_e_low(steps)
    stores = [
        pltpu.make_async_copy(ef.at[:, pl.ds(0, depth_x)], e_out, store_sem.at[0]),
        pltpu.make_async_copy(hf.at[:, pl.ds(1, depth_x)], h_out, store_sem.at[1]),
    ]
    for copy in stores:
        copy.start()
    read_out(ef[2, pl.ds(0, depth_x)], steps - 1)
    member = lax.broadcasted_iota(jnp.int32, (ports, slots), 0) == port_ref[...]
    member = jnp.where(member, 1.0, 0.0).astype(jnp.bfloat16)
    total = None
    for part in split_two(record[...]):
        piece = lax.dot_general(
            part, member, (((1,), (1,)), ((), ())), preferred_element_type=jnp.float32
        )
        total = piece if total is None else total + piece
    for row in range(steps):
        share[row] = total[row:row + 1, :]
    chunk = steps // count_y

    def spread(first, peers, source_of, target):
        moves = []
        for number, peer in enumerate(peers):
            moves.append(pltpu.make_async_remote_copy(
                src_ref=source_of(peer), dst_ref=target,
                send_sem=send_sum.at[first + number], recv_sem=recv_sum.at[first + number],
                device_id=peer, device_id_type=MESH))
            moves[-1].start()
        return moves

    def settle(moves):
        for move in moves:
            move.wait()

    mine = pl.ds(iy * chunk, chunk)
    moves = spread(
        0, line_y, lambda peer: share.at[pl.ds(peer[1] * chunk, chunk)], from_y.at[iy]
    )
    from_y[iy] = share[mine]
    settle(moves)
    from_x[ix] = sum(from_y[j] for j in range(count_y))
    first = len(line_y)
    settle(spread(first, line_x, lambda peer: from_x.at[ix], from_x.at[ix]))
    result[mine] = sum(from_x[i] for i in range(count_x))
    first = first + len(line_x)
    settle(spread(first, line_y, lambda peer: result.at[mine], result.at[mine]))
    for row in range(steps):
        power_ref[row:row + 1, :] = result[row]
    for copy in stores:
        copy.wait()


def local(
    electric, magnetic, aux_electric, aux_magnetic, grades, permittivity,
    dipole_cell, dipole_port, live_count, injection, waveform,
):
    depth_x, depth_y, depth_z = permittivity.shape
    slots = dipole_cell.shape[1]
    ports, steps = waveform.shape
    block = (depth_x, depth_y, depth_z)
    cells = depth_x * depth_y
    f32 = jnp.float32
    count_x, count_y = lax.axis_size("gx"), lax.axis_size("gy")
    chunk = steps // count_y
    assert chunk * count_y == steps
    transfers = count_x + 2 * count_y
    half = depth_y // 2
    row = (2, depth_x, depth_z)
    side = (2, half, depth_z)
    pair = (2, depth_z)
    messages = (row, row, side, side, side, side, pair, pair)
    tall, wide, single = (depth_x + 8, depth_z), (depth_y + 8, depth_z), (8, depth_z)
    coefficients = (tall, tall, wide, wide, single, single)
    shapes = (
        messages + tuple((SLOTS,) + shape for shape in messages) + coefficients + coefficients
        + (row,) * 4 + (side,) * 4 + ((40, depth_z),) + ((depth_x, half, depth_z),) * 4
    )
    scratch = [pltpu.VMEM(shape, f32) for shape in shapes]
    vmem = pl.BlockSpec(memory_space=pltpu.VMEM)
    anywhere = pl.BlockSpec(memory_space=pltpu.HBM)
    electric, magnetic, power = pl.pallas_call(
        kernel,
        out_shape=(
            jax.ShapeDtypeStruct(electric.shape, f32),
            jax.ShapeDtypeStruct(magnetic.shape, f32),
            jax.ShapeDtypeStruct((steps, ports), f32),
        ),
        in_specs=[anywhere] * 4 + [vmem] * 4
        + [pl.BlockSpec(memory_space=pltpu.SMEM)] + [vmem] * 2,
        out_specs=(anywhere, anywhere, vmem),
        scratch_shapes=[
            pltpu.VMEM((3, depth_x + 1, depth_y, depth_z), f32),
            pltpu.VMEM((3, depth_x + 1, depth_y, depth_z), f32),
            pltpu.VMEM((6,) + block, f32),
            pltpu.VMEM((6,) + block, f32),
            pltpu.VMEM((3,) + block, f32),
            pltpu.VMEM((3,) + block, f32),
            pltpu.VMEM(block, f32),
            pltpu.VMEM(block, f32),
            *scratch,
            pltpu.VMEM((cells, slots), jnp.bfloat16),
            pltpu.VMEM((cells, slots), f32),
            pltpu.VMEM((depth_z, slots), jnp.bfloat16),
            pltpu.VMEM((slots, depth_z), jnp.bfloat16),
            pltpu.VMEM((steps, slots), f32),
            pltpu.VMEM((steps, slots), f32),
            pltpu.VMEM(block, f32),
            pltpu.VMEM((steps, 1, ports), f32),
            pltpu.VMEM((count_y, chunk, 1, ports), f32),
            pltpu.VMEM((count_x, chunk, 1, ports), f32),
            pltpu.VMEM((steps, 1, ports), f32),
            pltpu.SemaphoreType.DMA((4,)),
            pltpu.SemaphoreType.DMA((2,)),
            pltpu.SemaphoreType.DMA((len(KINDS),)),
            pltpu.SemaphoreType.DMA((len(KINDS), SLOTS)),
            pltpu.SemaphoreType.DMA((len(COEFFICIENTS),)),
            pltpu.SemaphoreType.DMA((len(COEFFICIENTS),)),
            pltpu.SemaphoreType.DMA((transfers,)),
            pltpu.SemaphoreType.DMA((transfers,)),
        ],
        compiler_params=pltpu.CompilerParams(
            collective_id=0, has_side_effects=True, vmem_limit_bytes=60 * 1024 * 1024
        ),
    )(
        electric, magnetic, aux_electric, aux_magnetic, grades, permittivity,
        dipole_cell, dipole_port.reshape(1, slots), live_count, injection, waveform.T,
    )
    return electric, magnetic, power


def solution(mesh):
    in_specs = (
        P(None, "gx", "gy", None),
        P(None, "gx", "gy", None),
        P(None, "gx", "gy", None),
        P(None, "gx", "gy", None),
        P(None, "gx", "gy", None),
        P("gx", "gy", None),
        P(None, ("gx", "gy")),
        P(("gx", "gy")),
        P(("gx", "gy")),
        P(("gx", "gy"), None),
        P(),
    )
    out_specs = (P(None, "gx", "gy", None), P(None, "gx", "gy", None), P())
    return jax.shard_map(local, mesh=mesh, in_specs=in_specs, out_specs=out_specs, check_vma=False)
```

time: 148 us -> 75.8 us (0.51)
  Pallas kernels: 143 us -> 70.7 us
    pallas_call x1, Pallas kernels: 143 us -> 70.7 us  [local(): pl.pallas_call(kernel, out_shape=(jax.ShapeDtypeStruct(electric.shape, f3...]
where the time goes in v1:
time: 75.8 us; the launch traced here: 75.6 us
  Pallas kernels  70.7 us (93%)
  local copies, waits for them, and re-layouts  3.64 us (5%)
  between operations  1.31 us (2%)
    pallas_call x1, Pallas kernels, local(): pl.pallas_call(kernel, out_shape=(jax.ShapeDtypeStruct(electric.shape, f3...  70.7 us
    unnamed x7, local copies, waits for them, and re-layouts  3.64 us

profile of v1, /device:TPU:0, one launch (start us, length us, event | category | flops | bytes accessed | tf_op | source)
XLA Modules:
  0.0 75.6 jit_solution(11284386495438675579)
XLA Ops:
  1.3 70.7 %shard_map.130 = (f32[3,16,16,256]{3,2,1,0:T(8,128)}, f32[3,16,16,256]{3,2,1,0:T(8,128)}, f32[16,512]{1,0:T(8,128)}) custom-call(f32[3,16,16,256]{3,2,1,0:T(8,128)} %e_in.1, f32[3,16,16,256]{3,2,1,0:T(8,128)} %h_in.1, f32[6,16,16,256]{3,2,1,0:T(8,128)} %me_in.1, f32[6,16,16,256]{3,2,1,0:T(8,128)} %mh_in.1, s32[3,16,16,256]{3,2,1,0:T(8,128)} %grades_ref.1, ...), custom_call_target="tpu_custom_call" | custom-call | tf_op jit(solution)/shard_map/pallas_call | solution.py:512
  71.9 0.0 copy-start
  72.0 0.0 copy-start.1
  72.0 2.1 %copy.18 = f32[3,16,16,256]{3,2,1,0:T(8,128)} copy(f32[3,16,16,256]{3,2,1,0:T(8,128)} %get-tuple-element.6) | data formatting | bytes 1572864
  74.1 0.0 copy-done
  74.1 0.9 %copy.19 = f32[3,16,16,256]{3,2,1,0:T(8,128)} copy(f32[3,16,16,256]{3,2,1,0:T(8,128)S(1)} %copy-done) | data formatting | bytes 1572864
  75.0 0.0 copy-done.1
  75.0 0.6 copy.20
Async XLA Ops:
  71.9 2.2 %copy-start = (f32[3,16,16,256]{3,2,1,0:T(8,128)S(1)}, f32[3,16,16,256]{3,2,1,0:T(8,128)}, u32[]{:S(2)}) copy-start(f32[3,16,16,256]{3,2,1,0:T(8,128)} %get-tuple-element.7) | copy-start | bytes 2359300
  72.0 3.0 %copy-start.1 = (f32[16,512]{1,0:T(8,128)S(1)}, f32[16,512]{1,0:T(8,128)}, u32[]{:S(2)}) copy-start(f32[16,512]{1,0:T(8,128)} %get-tuple-element.8) | copy-start | bytes 98308

commit v2 on v1

--- a/solution.py
+++ b/solution.py
@@ -12,7 +12,8 @@
 absorb_keep = (0.0, 0.92, 0.75, 0.45)
 absorb_take = (0.0, -0.06, -0.18, -0.35)
 derivative_pairs = ((2, 1), (1, 2), (0, 2), (2, 0), (1, 0), (0, 1))
-UNROLL = 4
+UNROLL = 8
+TAIL = 4
 
 
 def grade_table(grades, table):
@@ -39,7 +40,7 @@
 def kernel(
     e_in, h_in, me_in, mh_in, grades_ref, eps_ref, cell_ref, port_ref, live_ref, inj_ref, wave_ref,
     e_out, h_out, power_ref,
-    ef, hf, me, mh, keep, take, factor, source,
+    ef, hf, me, mh, grades, eps, inj, keep, take, factor, source, member,
     say, sby, saxh, saxl, sbxl, sbxh, sd1, sd2,
     ray, rby, raxh, raxl, rbxl, rbxh, rd1, rd2,
     cs_up, cs_down, cs_right, cs_left, cs_d1, cs_d2,
@@ -47,8 +48,8 @@
     row_h, row_e, save_row_h, save_row_e, save_h_lo, save_h_hi, save_e_lo, save_e_hi, lines,
     edge_h, edge_ht, edge_e, edge_et,
     cell_t, cell_f, depth_t, depth, current, record, z_copy,
-    share, from_y, from_x, result,
-    load_sem, store_sem, send_sem, recv_sem, send_one, recv_one, send_sum, recv_sum,
+    share, from_y, from_x, result, late, late_y, late_x,
+    load_sem, store_sem, send_sem, recv_sem, send_one, recv_one, send_sum, recv_sum, send_late, recv_late,
 ):
     depth_x, depth_y, depth_z = eps_ref.shape
     ports, slots = inj_ref.shape[1], inj_ref.shape[0]
@@ -68,13 +69,17 @@
         return found
 
     loads = [
+        pltpu.make_async_copy(grades_ref, grades, load_sem.at[4]),
+        pltpu.make_async_copy(eps_ref, eps, load_sem.at[5]),
         pltpu.make_async_copy(e_in, ef.at[:, pl.ds(0, depth_x)], load_sem.at[0]),
         pltpu.make_async_copy(h_in, hf.at[:, pl.ds(1, depth_x)], load_sem.at[1]),
         pltpu.make_async_copy(me_in, me, load_sem.at[2]),
         pltpu.make_async_copy(mh_in, mh, load_sem.at[3]),
+        pltpu.make_async_copy(inj_ref, inj, load_sem.at[6]),
     ]
     for copy in loads:
         copy.start()
+    record[...] = jnp.zeros(record.shape, f32)
 
     plane = jnp.zeros((depth_y, depth_z), f32)
     for component in range(3):
@@ -99,12 +104,14 @@
 
     def prepare(x, _):
         for d in range(3):
-            level = grades_ref[d, x]
+            level = grades[d, x]
             keep[d, x] = grade_table(level, absorb_keep)
             take[d, x] = grade_table(level, absorb_take)
-        factor[x] = courant / eps_ref[x]
+        factor[x] = courant / eps[x]
         return 0
 
+    for copy in loads[:2]:
+        copy.wait()
     lax.fori_loop(0, depth_x, prepare, 0)
 
     row_half = lax.broadcasted_iota(jnp.int32, (half, depth_z), 0)
@@ -361,24 +368,6 @@
         chosen = jnp.sum(picked * cell_f[...], axis=0, keepdims=True)
         record[pl.ds(step, 1), :] = chosen * current[pl.ds(step, 1), :]
 
-    pl.semaphore_wait(barrier, len(line_x) + len(line_y) + len(across))
-    for wanted, _, copy in once:
-        pl.when(wanted)(copy.start)
-    for copy in loads:
-        copy.wait()
-
-    for x in range(depth_x):
-        sby[0, x:x + 1, :] = ef[0, x, 0:1, :]
-        sby[1, x:x + 1, :] = ef[2, x, 0:1, :]
-    for c in (1, 2):
-        sbxl[c - 1] = ef[c, 0, low]
-        sbxh[c - 1] = ef[c, 0, high]
-    sd2[1:2, :] = ef[0, last_x, 0:1, :]
-    send(0, "by", "bxl", "bxh", "d2")
-    save_row_e[...] = sby[...]
-    save_e_lo[...] = sbxl[...]
-    save_e_hi[...] = sbxh[...]
-
     cells = (cell_ref[0:1, :] - ix * depth_x) * depth_y + (cell_ref[1:2, :] - iy * depth_y)
     hit = lax.broadcasted_iota(jnp.int32, cell_f.shape, 0) == cells
     cell_f[...] = jnp.where(hit, 1.0, 0.0)
@@ -388,13 +377,90 @@
     depth_t[...] = table.astype(jnp.bfloat16)
     depth[...] = table.T.astype(jnp.bfloat16)
     live = lax.broadcasted_iota(jnp.int32, (1, slots), 1) < live_ref[0]
+    loads[6].wait()
     flow = lax.dot_general(
-        wave_ref[...], inj_ref[...], (((1,), (1,)), ((), ())), preferred_element_type=jnp.float32
+        wave_ref[...], inj[...], (((1,), (1,)), ((), ())), preferred_element_type=jnp.float32
     )
     current[...] = jnp.where(live, flow, 0.0)
-    for wanted, expected, copy in once:
-        pl.when(wanted)(copy.wait_send)
-        pl.when(expected)(copy.wait_recv)
+    hit = lax.broadcasted_iota(jnp.int32, (ports, slots), 0) == port_ref[...]
+    member[...] = jnp.where(hit, 1.0, 0.0).astype(jnp.bfloat16)
+    for copy in loads[2:6]:
+        copy.wait()
+
+    for x in range(depth_x):
+        sby[0, x:x + 1, :] = ef[0, x, 0:1, :]
+        sby[1, x:x + 1, :] = ef[2, x, 0:1, :]
+    for c in (1, 2):
+        sbxl[c - 1] = ef[c, 0, low]
+        sbxh[c - 1] = ef[c, 0, high]
+    sd2[1:2, :] = ef[0, last_x, 0:1, :]
+    pl.semaphore_wait(barrier, len(line_x) + len(line_y) + len(across))
+    for wanted, _, copy in once:
+        pl.when(wanted)(copy.start)
+    send(0, "by", "bxl", "bxh", "d2")
+    save_row_e[...] = sby[...]
+    save_e_lo[...] = sbxl[...]
+    save_e_hi[...] = sbxh[...]
+
+
+    def port_sums():
+        total = None
+        for part in split_two(record[...]):
+            piece = lax.dot_general(
+                part, member[...], (((1,), (1,)), ((), ())), preferred_element_type=f32
+            )
+            total = piece if total is None else total + piece
+        return total
+
+    chunk = steps // count_y
+    mine = pl.ds(iy * chunk, chunk)
+
+    def spread(sems, first, peers, source_of, target):
+        return [
+            pltpu.make_async_remote_copy(
+                src_ref=source_of(peer), dst_ref=target,
+                send_sem=sems[0].at[first + number], recv_sem=sems[1].at[first + number],
+                device_id=peer, device_id_type=MESH)
+            for number, peer in enumerate(peers)
+        ]
+
+    def launch(moves):
+        for move in moves:
+            move.start()
+
+    def settle(moves):
+        for move in moves:
+            move.wait()
+
+    sums = (send_sum, recv_sum)
+
+    def first_moves():
+        return spread(
+            sums, 0, line_y, lambda peer: share.at[pl.ds(peer[1] * chunk, chunk)], from_y.at[iy])
+
+    def second_moves():
+        return spread(sums, len(line_y), line_x, lambda peer: from_x.at[ix], from_x.at[ix])
+
+    def third_moves():
+        first = len(line_y) + len(line_x)
+        return spread(sums, first, line_y, lambda peer: result.at[mine], result.at[mine])
+
+    def reduce_one():
+        total = port_sums()
+        for row in range(steps):
+            share[row] = total[row:row + 1, :]
+        launch(first_moves())
+        from_y[iy] = share[mine]
+
+    def reduce_two():
+        settle(first_moves())
+        from_x[ix] = sum(from_y[j] for j in range(count_y))
+        launch(second_moves())
+
+    def reduce_three():
+        settle(second_moves())
+        result[mine] = sum(from_x[i] for i in range(count_x))
+        launch(third_moves())
 
     def turn(step, _):
         more = step < steps
@@ -411,6 +477,13 @@
             saxl[c - 1] = hf[c, depth_x, low]
         send(step, "axl")
         sent(step - 1, "by", "bxl", "d2")
+
+        @pl.when(step == 1)
+        def _():
+            for wanted, expected, copy in once:
+                pl.when(wanted)(copy.wait_send)
+                pl.when(expected)(copy.wait_recv)
+
         settle_h_low(step - 1)
         update_e(False)
         for c in (1, 2):
@@ -418,6 +491,9 @@
         sd2[1:2, :] = sby[0, last_x:depth_x, :]
         pl.when(more)(lambda: send(step, "d2", "by", "bxl"))
         read_out(z_copy[...], lax.rem(step + steps - 2, steps))
+        pl.when(step == steps - TAIL + 1)(reduce_one)
+        pl.when(step == steps - TAIL + 3)(reduce_two)
+        pl.when(step == steps - TAIL + 4)(reduce_three)
         sent(step - 1, "bxh")
         settle_h_high(step - 1)
         update_e(True)
@@ -437,46 +513,20 @@
     for copy in stores:
         copy.start()
     read_out(ef[2, pl.ds(0, depth_x)], steps - 1)
-    member = lax.broadcasted_iota(jnp.int32, (ports, slots), 0) == port_ref[...]
-    member = jnp.where(member, 1.0, 0.0).astype(jnp.bfloat16)
-    total = None
-    for part in split_two(record[...]):
-        piece = lax.dot_general(
-            part, member, (((1,), (1,)), ((), ())), preferred_element_type=jnp.float32
-        )
-        total = piece if total is None else total + piece
-    for row in range(steps):
-        share[row] = total[row:row + 1, :]
-    chunk = steps // count_y
-
-    def spread(first, peers, source_of, target):
-        moves = []
-        for number, peer in enumerate(peers):
-            moves.append(pltpu.make_async_remote_copy(
-                src_ref=source_of(peer), dst_ref=target,
-                send_sem=send_sum.at[first + number], recv_sem=recv_sum.at[first + number],
-                device_id=peer, device_id_type=MESH))
-            moves[-1].start()
-        return moves
-
-    def settle(moves):
-        for move in moves:
-            move.wait()
-
-    mine = pl.ds(iy * chunk, chunk)
-    moves = spread(
-        0, line_y, lambda peer: share.at[pl.ds(peer[1] * chunk, chunk)], from_y.at[iy]
-    )
-    from_y[iy] = share[mine]
+    late[...] = port_sums()[steps - TAIL:, :]
+    lates = (send_late, recv_late)
+    moves = spread(lates, 0, line_y, lambda peer: late, late_y.at[iy])
+    launch(moves)
+    late_y[iy] = late[...]
+    settle(third_moves())
+    for row in range(steps - TAIL):
+        power_ref[row:row + 1, :] = result[row]
     settle(moves)
-    from_x[ix] = sum(from_y[j] for j in range(count_y))
-    first = len(line_y)
-    settle(spread(first, line_x, lambda peer: from_x.at[ix], from_x.at[ix]))
-    result[mine] = sum(from_x[i] for i in range(count_x))
-    first = first + len(line_x)
-    settle(spread(first, line_y, lambda peer: result.at[mine], result.at[mine]))
-    for row in range(steps):
-        power_ref[row:row + 1, :] = result[row]
+    late_x[ix] = sum(late_y[j] for j in range(count_y))
+    moves = spread(lates, len(line_y), line_x, lambda peer: late_x.at[ix], late_x.at[ix])
+    launch(moves)
+    settle(moves)
+    power_ref[steps - TAIL:, :] = sum(late_x[i] for i in range(count_x))
     for copy in stores:
         copy.wait()
 
@@ -516,18 +566,22 @@
             jax.ShapeDtypeStruct(magnetic.shape, f32),
             jax.ShapeDtypeStruct((steps, ports), f32),
         ),
-        in_specs=[anywhere] * 4 + [vmem] * 4
-        + [pl.BlockSpec(memory_space=pltpu.SMEM)] + [vmem] * 2,
+        in_specs=[anywhere] * 6 + [vmem] * 2
+        + [pl.BlockSpec(memory_space=pltpu.SMEM), anywhere, vmem],
         out_specs=(anywhere, anywhere, vmem),
         scratch_shapes=[
             pltpu.VMEM((3, depth_x + 1, depth_y, depth_z), f32),
             pltpu.VMEM((3, depth_x + 1, depth_y, depth_z), f32),
             pltpu.VMEM((6,) + block, f32),
             pltpu.VMEM((6,) + block, f32),
+            pltpu.VMEM((3,) + block, jnp.int32),
+            pltpu.VMEM(block, f32),
+            pltpu.VMEM((slots, ports), jnp.bfloat16),
             pltpu.VMEM((3,) + block, f32),
             pltpu.VMEM((3,) + block, f32),
             pltpu.VMEM(block, f32),
             pltpu.VMEM(block, f32),
+            pltpu.VMEM((ports, slots), jnp.bfloat16),
             *scratch,
             pltpu.VMEM((cells, slots), jnp.bfloat16),
             pltpu.VMEM((cells, slots), f32),
@@ -540,7 +594,10 @@
             pltpu.VMEM((count_y, chunk, 1, ports), f32),
             pltpu.VMEM((count_x, chunk, 1, ports), f32),
             pltpu.VMEM((steps, 1, ports), f32),
-            pltpu.SemaphoreType.DMA((4,)),
+            pltpu.VMEM((TAIL, ports), f32),
+            pltpu.VMEM((count_y, TAIL, ports), f32),
+            pltpu.VMEM((count_x, TAIL, ports), f32),
+            pltpu.SemaphoreType.DMA((7,)),
             pltpu.SemaphoreType.DMA((2,)),
             pltpu.SemaphoreType.DMA((len(KINDS),)),
             pltpu.SemaphoreType.DMA((len(KINDS), SLOTS)),
@@ -548,6 +605,8 @@
             pltpu.SemaphoreType.DMA((len(COEFFICIENTS),)),
             pltpu.SemaphoreType.DMA((transfers,)),
             pltpu.SemaphoreType.DMA((transfers,)),
+            pltpu.SemaphoreType.DMA((count_x + count_y,)),
+            pltpu.SemaphoreType.DMA((count_x + count_y,)),
         ],
         compiler_params=pltpu.CompilerParams(
             collective_id=0, has_side_effects=True, vmem_limit_bytes=60 * 1024 * 1024

time: 75.8 us -> 68.7 us (0.906)
  Pallas kernels: 70.7 us -> 63.5 us
    pallas_call x1, Pallas kernels: 70.7 us -> 63.5 us  [local(): pl.pallas_call(kernel, out_shape=(jax.ShapeDtypeStruct(electric.shape, f3...]
where the time goes in v2:
time: 68.7 us; the launch traced here: 68.5 us
  Pallas kernels  63.5 us (92%)
  local copies, waits for them, and re-layouts  3.64 us (5%)
  between operations  1.31 us (2%)
    pallas_call x1, Pallas kernels, local(): pl.pallas_call(kernel, out_shape=(jax.ShapeDtypeStruct(electric.shape, f3...  63.5 us
    unnamed x7, local copies, waits for them, and re-layouts  3.64 us

profile of v2, /device:TPU:0, one launch (start us, length us, event | category | flops | bytes accessed | tf_op | source)
XLA Modules:
  0.0 68.5 jit_solution(11441141451550506346)
XLA Ops:
  1.3 63.5 %shard_map.130 = (f32[3,16,16,256]{3,2,1,0:T(8,128)}, f32[3,16,16,256]{3,2,1,0:T(8,128)}, f32[16,512]{1,0:T(8,128)}) custom-call(f32[3,16,16,256]{3,2,1,0:T(8,128)} %e_in.1, f32[3,16,16,256]{3,2,1,0:T(8,128)} %h_in.1, f32[6,16,16,256]{3,2,1,0:T(8,128)} %me_in.1, f32[6,16,16,256]{3,2,1,0:T(8,128)} %mh_in.1, s32[3,16,16,256]{3,2,1,0:T(8,128)} %grades_ref.1, ...), custom_call_target="tpu_custom_call" | custom-call | tf_op jit(solution)/shard_map/pallas_call | solution.py:562
  64.8 0.0 copy-start
  64.8 0.0 copy-start.1
  64.8 2.1 %copy.18 = f32[3,16,16,256]{3,2,1,0:T(8,128)} copy(f32[3,16,16,256]{3,2,1,0:T(8,128)} %get-tuple-element.6) | data formatting | bytes 1572864
  67.0 0.0 copy-done
  67.0 0.9 %copy.19 = f32[3,16,16,256]{3,2,1,0:T(8,128)} copy(f32[3,16,16,256]{3,2,1,0:T(8,128)S(1)} %copy-done) | data formatting | bytes 1572864
  67.8 0.0 copy-done.1
  67.8 0.6 copy.20
Async XLA Ops:
  64.8 2.2 %copy-start = (f32[3,16,16,256]{3,2,1,0:T(8,128)S(1)}, f32[3,16,16,256]{3,2,1,0:T(8,128)}, u32[]{:S(2)}) copy-start(f32[3,16,16,256]{3,2,1,0:T(8,128)} %get-tuple-element.7) | copy-start | bytes 2359300
  64.8 3.0 %copy-start.1 = (f32[16,512]{1,0:T(8,128)S(1)}, f32[16,512]{1,0:T(8,128)}, u32[]{:S(2)}) copy-start(f32[16,512]{1,0:T(8,128)} %get-tuple-element.8) | copy-start | bytes 98308

commit v3 on v2

--- a/solution.py
+++ b/solution.py
@@ -39,8 +39,8 @@
 
 def kernel(
     e_in, h_in, me_in, mh_in, grades_ref, eps_ref, cell_ref, port_ref, live_ref, inj_ref, wave_ref,
-    e_out, h_out, power_ref,
-    ef, hf, me, mh, grades, eps, inj, keep, take, factor, source, member,
+    ef, hf, power_ref,
+    me, mh, grades, eps, inj, keep, take, factor, source, member,
     say, sby, saxh, saxl, sbxl, sbxh, sd1, sd2,
     ray, rby, raxh, raxl, rbxl, rbxh, rd1, rd2,
     cs_up, cs_down, cs_right, cs_left, cs_d1, cs_d2,
@@ -49,7 +49,7 @@
     edge_h, edge_ht, edge_e, edge_et,
     cell_t, cell_f, depth_t, depth, current, record, z_copy,
     share, from_y, from_x, result, late, late_y, late_x,
-    load_sem, store_sem, send_sem, recv_sem, send_one, recv_one, send_sum, recv_sum, send_late, recv_late,
+    load_sem, send_sem, recv_sem, send_one, recv_one, send_sum, recv_sum, send_late, recv_late,
 ):
     depth_x, depth_y, depth_z = eps_ref.shape
     ports, slots = inj_ref.shape[1], inj_ref.shape[0]
@@ -69,12 +69,12 @@
         return found
 
     loads = [
-        pltpu.make_async_copy(grades_ref, grades, load_sem.at[4]),
-        pltpu.make_async_copy(eps_ref, eps, load_sem.at[5]),
         pltpu.make_async_copy(e_in, ef.at[:, pl.ds(0, depth_x)], load_sem.at[0]),
-        pltpu.make_async_copy(h_in, hf.at[:, pl.ds(1, depth_x)], load_sem.at[1]),
-        pltpu.make_async_copy(me_in, me, load_sem.at[2]),
-        pltpu.make_async_copy(mh_in, mh, load_sem.at[3]),
+        pltpu.make_async_copy(grades_ref, grades, load_sem.at[1]),
+        pltpu.make_async_copy(eps_ref, eps, load_sem.at[2]),
+        pltpu.make_async_copy(h_in, hf.at[:, pl.ds(1, depth_x)], load_sem.at[3]),
+        pltpu.make_async_copy(me_in, me, load_sem.at[4]),
+        pltpu.make_async_copy(mh_in, mh, load_sem.at[5]),
         pltpu.make_async_copy(inj_ref, inj, load_sem.at[6]),
     ]
     for copy in loads:
@@ -102,6 +102,59 @@
     for peer in line_x + line_y + across:
         pl.semaphore_signal(barrier, inc=1, device_id=peer, device_id_type=MESH)
 
+    once = []
+    for number, (source_ref, target_ref) in enumerate((
+        (cs_up, cr_up), (cs_down, cr_down), (cs_right, cr_right),
+        (cs_left, cr_left), (cs_d1, cr_d1), (cs_d2, cr_d2),
+    )):
+        dx, dy = COEFFICIENTS[number]
+        once.append((there(dx, dy), there(-dx, -dy), pltpu.make_async_remote_copy(
+            src_ref=source_ref, dst_ref=target_ref,
+            send_sem=send_one.at[number], recv_sem=recv_one.at[number],
+            device_id=(ix + dx, iy + dy), device_id_type=MESH)))
+
+    sends = dict(ay=say, by=sby, axh=saxh, axl=saxl, bxl=sbxl, bxh=sbxh, d1=sd1, d2=sd2)
+    gets = dict(ay=ray, by=rby, axh=raxh, axl=raxl, bxl=rbxl, bxh=rbxh, d1=rd1, d2=rd2)
+
+    def message(kind, step):
+        number = KINDS.index(kind)
+        slot = lax.rem(step, SLOTS)
+        dx, dy = TRAVEL[kind]
+        return pltpu.make_async_remote_copy(
+            src_ref=sends[kind], dst_ref=gets[kind].at[slot],
+            send_sem=send_sem.at[number], recv_sem=recv_sem.at[number, slot],
+            device_id=(ix + dx, iy + dy), device_id_type=MESH)
+
+    def send(step, *kinds):
+        for kind in kinds:
+            dx, dy = TRAVEL[kind]
+            pl.when(there(dx, dy))(message(kind, step).start)
+
+    def sent(step, *kinds):
+        for kind in kinds:
+            dx, dy = TRAVEL[kind]
+            pl.when(there(dx, dy))(message(kind, step).wait_send)
+
+    def arrived(step, *kinds):
+        for kind in kinds:
+            dx, dy = TRAVEL[kind]
+            pl.when(there(-dx, -dy))(message(kind, step).wait_recv)
+
+    low, high = slice(0, half), slice(half, depth_y)
+    loads[0].wait()
+
+    for x in range(depth_x):
+        sby[0, x:x + 1, :] = ef[0, x, 0:1, :]
+        sby[1, x:x + 1, :] = ef[2, x, 0:1, :]
+    for c in (1, 2):
+        sbxl[c - 1] = ef[c, 0, low]
+        sbxh[c - 1] = ef[c, 0, high]
+    sd2[1:2, :] = ef[0, last_x, 0:1, :]
+    pl.semaphore_wait(barrier, len(line_x) + len(line_y) + len(across))
+    send(0, "by", "bxl", "bxh", "d2")
+    save_row_e[...] = sby[...]
+    save_e_lo[...] = sbxl[...]
+    save_e_hi[...] = sbxh[...]
     def prepare(x, _):
         for d in range(3):
             level = grades[d, x]
@@ -110,7 +163,7 @@
         factor[x] = courant / eps[x]
         return 0
 
-    for copy in loads[:2]:
+    for copy in loads[1:3]:
         copy.wait()
     lax.fori_loop(0, depth_x, prepare, 0)
 
@@ -137,45 +190,8 @@
     cs_d1[0:1, :] = cs_up[0:1, :]
     cs_d2[0:1, :] = cs_down[last_x:depth_x, :]
 
-    once = []
-    for number, (source_ref, target_ref) in enumerate((
-        (cs_up, cr_up), (cs_down, cr_down), (cs_right, cr_right),
-        (cs_left, cr_left), (cs_d1, cr_d1), (cs_d2, cr_d2),
-    )):
-        dx, dy = COEFFICIENTS[number]
-        once.append((there(dx, dy), there(-dx, -dy), pltpu.make_async_remote_copy(
-            src_ref=source_ref, dst_ref=target_ref,
-            send_sem=send_one.at[number], recv_sem=recv_one.at[number],
-            device_id=(ix + dx, iy + dy), device_id_type=MESH)))
-
-    sends = dict(ay=say, by=sby, axh=saxh, axl=saxl, bxl=sbxl, bxh=sbxh, d1=sd1, d2=sd2)
-    gets = dict(ay=ray, by=rby, axh=raxh, axl=raxl, bxl=rbxl, bxh=rbxh, d1=rd1, d2=rd2)
-
-    def message(kind, step):
-        number = KINDS.index(kind)
-        slot = lax.rem(step, SLOTS)
-        dx, dy = TRAVEL[kind]
-        return pltpu.make_async_remote_copy(
-            src_ref=sends[kind], dst_ref=gets[kind].at[slot],
-            send_sem=send_sem.at[number], recv_sem=recv_sem.at[number, slot],
-            device_id=(ix + dx, iy + dy), device_id_type=MESH)
-
-    def send(step, *kinds):
-        for kind in kinds:
-            dx, dy = TRAVEL[kind]
-            pl.when(there(dx, dy))(message(kind, step).start)
-
-    def sent(step, *kinds):
-        for kind in kinds:
-            dx, dy = TRAVEL[kind]
-            pl.when(there(dx, dy))(message(kind, step).wait_send)
-
-    def arrived(step, *kinds):
-        for kind in kinds:
-            dx, dy = TRAVEL[kind]
-            pl.when(there(-dx, -dy))(message(kind, step).wait_recv)
-
-    low, high = slice(0, half), slice(half, depth_y)
+    for wanted, _, copy in once:
+        pl.when(wanted)(copy.start)
     lanes = lax.broadcasted_iota(jnp.int32, (half, depth_z), 1)
     z_last, z_first = lanes == depth_z - 1, lanes == 0
 
@@ -297,31 +313,39 @@
         save_e_lo[0] = ef[1, 0, low]
         save_e_lo[1] = ef[2, 0, low]
 
-    def settle_h_low(step):
+    def settle_h_low(step, first):
         arrived(step, "bxl")
         slot = lax.rem(step, SLOTS)
-        scale = cr_left[low]
-        side_y = rbxl[slot, 0] + scale * save_h_lo[1]
-        side_z = rbxl[slot, 1] - scale * save_h_lo[0]
-        corner = cr_left[depth_y:depth_y + 1, :] * lines[hx_corner]
-        side_z = side_z + jnp.where(is_bottom, corner, 0.0)
+        side_y, side_z = rbxl[slot, 0], rbxl[slot, 1]
+        if not first:
+            scale = cr_left[low]
+            side_y = side_y + scale * save_h_lo[1]
+            side_z = side_z - scale * save_h_lo[0]
+            corner = cr_left[depth_y:depth_y + 1, :] * lines[hx_corner]
+            side_z = side_z + jnp.where(is_bottom, corner, 0.0)
         lines[ez_edge] = side_z[0:1, :]
         fix_h_side(low, side_y, side_z)
         save_h_lo[0] = hf[1, depth_x, low]
         save_h_lo[1] = hf[2, depth_x, low]
         sd2[0:1, :] = hf[1, depth_x, 0:1, :]
 
-    def settle_h_high(step):
+    def settle_h_high(step, first):
         arrived(step, "by", "d2", "bxh")
         slot = lax.rem(step, SLOTS)
-        scale = cr_down[rows_x]
-        row_e[0] = rby[slot, 0] - scale * save_row_h[1]
-        row_e[1] = rby[slot, 1] + scale * save_row_h[0]
-        row_e[1, 0:1, :] = row_e[1, 0:1, :] - cr_down[depth_x:depth_x + 1, :] * rd2[slot, 0:1, :]
-        scale = cr_left[high]
-        side_y = rbxh[slot, 0] + scale * save_h_hi[1]
-        side_z = rbxh[slot, 1] - scale * save_h_hi[0]
-        lines[ex_corner] = rd2[slot, 1:2, :] - cr_d2[0:1, :] * lines[hz_edge]
+        side_y, side_z = rbxh[slot, 0], rbxh[slot, 1]
+        if first:
+            row_e[...] = rby[slot]
+            lines[ex_corner] = rd2[slot, 1:2, :]
+        else:
+            scale = cr_down[rows_x]
+            row_e[0] = rby[slot, 0] - scale * save_row_h[1]
+            row_e[1] = rby[slot, 1] + scale * save_row_h[0]
+            row_e[1, 0:1, :] = (
+                row_e[1, 0:1, :] - cr_down[depth_x:depth_x + 1, :] * rd2[slot, 0:1, :])
+            scale = cr_left[high]
+            side_y = side_y + scale * save_h_hi[1]
+            side_z = side_z - scale * save_h_hi[0]
+            lines[ex_corner] = rd2[slot, 1:2, :] - cr_d2[0:1, :] * lines[hz_edge]
         fix_h_side(high, side_y, side_z)
         for x in range(depth_x):
             line_ex, line_ez = row_e[0, x:x + 1, :], row_e[1, x:x + 1, :]
@@ -384,24 +408,10 @@
     current[...] = jnp.where(live, flow, 0.0)
     hit = lax.broadcasted_iota(jnp.int32, (ports, slots), 0) == port_ref[...]
     member[...] = jnp.where(hit, 1.0, 0.0).astype(jnp.bfloat16)
-    for copy in loads[2:6]:
+
+
+    for copy in loads[3:6]:
         copy.wait()
-
-    for x in range(depth_x):
-        sby[0, x:x + 1, :] = ef[0, x, 0:1, :]
-        sby[1, x:x + 1, :] = ef[2, x, 0:1, :]
-    for c in (1, 2):
-        sbxl[c - 1] = ef[c, 0, low]
-        sbxh[c - 1] = ef[c, 0, high]
-    sd2[1:2, :] = ef[0, last_x, 0:1, :]
-    pl.semaphore_wait(barrier, len(line_x) + len(line_y) + len(across))
-    for wanted, _, copy in once:
-        pl.when(wanted)(copy.start)
-    send(0, "by", "bxl", "bxh", "d2")
-    save_row_e[...] = sby[...]
-    save_e_lo[...] = sbxl[...]
-    save_e_hi[...] = sbxh[...]
-
 
     def port_sums():
         total = None
@@ -478,13 +488,8 @@
         send(step, "axl")
         sent(step - 1, "by", "bxl", "d2")
 
-        @pl.when(step == 1)
-        def _():
-            for wanted, expected, copy in once:
-                pl.when(wanted)(copy.wait_send)
-                pl.when(expected)(copy.wait_recv)
-
-        settle_h_low(step - 1)
+        pl.when(step == 1)(lambda: settle_h_low(step - 1, True))
+        pl.when(step > 1)(lambda: settle_h_low(step - 1, False))
         update_e(False)
         for c in (1, 2):
             sbxl[c - 1] = ef[c, 0, low]
@@ -495,23 +500,25 @@
         pl.when(step == steps - TAIL + 3)(reduce_two)
         pl.when(step == steps - TAIL + 4)(reduce_three)
         sent(step - 1, "bxh")
-        settle_h_high(step - 1)
+        pl.when(step == 1)(lambda: settle_h_high(step - 1, True))
+        pl.when(step > 1)(lambda: settle_h_high(step - 1, False))
         update_e(True)
         for c in (1, 2):
             sbxh[c - 1] = ef[c, 0, high]
         pl.when(more)(lambda: send(step, "bxh"))
         sent(step, "ay", "axh", "d1", "axl")
+
+        @pl.when(step == 1)
+        def _():
+            for wanted, expected, copy in once:
+                pl.when(wanted)(copy.wait_send)
+                pl.when(expected)(copy.wait_recv)
+
         settle_e_high(step)
         return 0
 
     lax.fori_loop(1, steps + 1, turn, 0)
     settle_e_low(steps)
-    stores = [
-        pltpu.make_async_copy(ef.at[:, pl.ds(0, depth_x)], e_out, store_sem.at[0]),
-        pltpu.make_async_copy(hf.at[:, pl.ds(1, depth_x)], h_out, store_sem.at[1]),
-    ]
-    for copy in stores:
-        copy.start()
     read_out(ef[2, pl.ds(0, depth_x)], steps - 1)
     late[...] = port_sums()[steps - TAIL:, :]
     lates = (send_late, recv_late)
@@ -527,7 +534,18 @@
     launch(moves)
     settle(moves)
     power_ref[steps - TAIL:, :] = sum(late_x[i] for i in range(count_x))
-    for copy in stores:
+
+
+def store_kernel(ef, hf, power_ref, e_out, h_out, power_out, sem):
+    depth_x = e_out.shape[1]
+    copies = [
+        pltpu.make_async_copy(ef.at[:, pl.ds(0, depth_x)], e_out, sem.at[0]),
+        pltpu.make_async_copy(hf.at[:, pl.ds(1, depth_x)], h_out, sem.at[1]),
+        pltpu.make_async_copy(power_ref, power_out, sem.at[2]),
+    ]
+    for copy in copies:
+        copy.start()
+    for copy in copies:
         copy.wait()
 
 
@@ -559,19 +577,17 @@
     scratch = [pltpu.VMEM(shape, f32) for shape in shapes]
     vmem = pl.BlockSpec(memory_space=pltpu.VMEM)
     anywhere = pl.BlockSpec(memory_space=pltpu.HBM)
-    electric, magnetic, power = pl.pallas_call(
+    fields = pl.pallas_call(
         kernel,
         out_shape=(
-            jax.ShapeDtypeStruct(electric.shape, f32),
-            jax.ShapeDtypeStruct(magnetic.shape, f32),
-            jax.ShapeDtypeStruct((steps, ports), f32),
+            pltpu.VMEM((3, depth_x + 1, depth_y, depth_z), f32),
+            pltpu.VMEM((3, depth_x + 1, depth_y, depth_z), f32),
+            pltpu.VMEM((steps, ports), f32),
         ),
         in_specs=[anywhere] * 6 + [vmem] * 2
         + [pl.BlockSpec(memory_space=pltpu.SMEM), anywhere, vmem],
-        out_specs=(anywhere, anywhere, vmem),
+        out_specs=(vmem, vmem, vmem),
         scratch_shapes=[
-            pltpu.VMEM((3, depth_x + 1, depth_y, depth_z), f32),
-            pltpu.VMEM((3, depth_x + 1, depth_y, depth_z), f32),
             pltpu.VMEM((6,) + block, f32),
             pltpu.VMEM((6,) + block, f32),
             pltpu.VMEM((3,) + block, jnp.int32),
@@ -598,7 +614,6 @@
             pltpu.VMEM((count_y, TAIL, ports), f32),
             pltpu.VMEM((count_x, TAIL, ports), f32),
             pltpu.SemaphoreType.DMA((7,)),
-            pltpu.SemaphoreType.DMA((2,)),
             pltpu.SemaphoreType.DMA((len(KINDS),)),
             pltpu.SemaphoreType.DMA((len(KINDS), SLOTS)),
             pltpu.SemaphoreType.DMA((len(COEFFICIENTS),)),
@@ -615,7 +630,18 @@
         electric, magnetic, aux_electric, aux_magnetic, grades, permittivity,
         dipole_cell, dipole_port.reshape(1, slots), live_count, injection, waveform.T,
     )
-    return electric, magnetic, power
+    return pl.pallas_call(
+        store_kernel,
+        out_shape=(
+            jax.ShapeDtypeStruct(electric.shape, f32),
+            jax.ShapeDtypeStruct(magnetic.shape, f32),
+            jax.ShapeDtypeStruct((steps, ports), f32),
+        ),
+        in_specs=[vmem] * 3,
+        out_specs=(anywhere,) * 3,
+        scratch_shapes=[pltpu.SemaphoreType.DMA((3,))],
+        compiler_params=pltpu.CompilerParams(vmem_limit_bytes=1024 * 1024),
+    )(*fields)
 
 
 def solution(mesh):

time: 68.7 us -> 63.6 us (0.926)
  local copies, waits for them, and re-layouts: 3.64 us -> 0 us
  Pallas kernels: 63.5 us -> 62 us
    unnamed x7 -> x0, local copies, waits for them, and re-layouts: 3.64 us -> none
    pallas_call x1 -> x2, Pallas kernels: 63.5 us -> 62 us  [the longest x1 60.9 us: local(): pl.pallas_call(kernel, out_shape=(pltpu.VMEM((3, depth_x + 1, depth_y, de...]
where the time goes in v3:
time: 63.6 us; the launch traced here: 63.3 us
  Pallas kernels  62 us (97%)
  between operations  1.29 us (2%)
    pallas_call x1, Pallas kernels, local(): pl.pallas_call(kernel, out_shape=(pltpu.VMEM((3, depth_x + 1, depth_y, de...  60.9 us

profile of v3, /device:TPU:0, one launch (start us, length us, event | category | flops | bytes accessed | tf_op | source)
XLA Modules:
  0.0 63.3 jit_solution(16318159596138146881)
XLA Ops:
  1.3 60.9 %shard_map.130 = (f32[3,17,16,256]{3,2,1,0:T(8,128)S(1)}, f32[3,17,16,256]{3,2,1,0:T(8,128)S(1)}, f32[16,512]{1,0:T(8,128)S(1)}) custom-call(f32[3,16,16,256]{3,2,1,0:T(8,128)} %e_in.1, f32[3,16,16,256]{3,2,1,0:T(8,128)} %h_in.1, f32[6,16,16,256]{3,2,1,0:T(8,128)} %me_in.1, f32[6,16,16,256]{3,2,1,0:T(8,128)} %mh_in.1, s32[3,16,16,256]{3,2,1,0:T(8,128)} %grades_ref.1, ...), custom_call_target="tpu_custom_call" | custom-call | tf_op jit(solution)/shard_map/pallas_call | solution.py:580
  62.1 1.2 %shard_map.131 = (f32[3,16,16,256]{3,2,1,0:T(8,128)}, f32[3,16,16,256]{3,2,1,0:T(8,128)}, f32[16,512]{1,0:T(8,128)}) custom-call(f32[3,17,16,256]{3,2,1,0:T(8,128)S(1)} %get-tuple-element.6.ef, f32[3,17,16,256]{3,2,1,0:T(8,128)S(1)} %get-tuple-element.7.hf, f32[16,512]{1,0:T(8,128)S(1)} %get-tuple-element.8.power_ref), custom_call_target="tpu_custom_call" | custom-call | tf_op jit(solution)/shard_map/pallas_call | solution.py:633

commit v4 on v3

--- a/solution.py
+++ b/solution.py
@@ -12,7 +12,6 @@
 absorb_keep = (0.0, 0.92, 0.75, 0.45)
 absorb_take = (0.0, -0.06, -0.18, -0.35)
 derivative_pairs = ((2, 1), (1, 2), (0, 2), (2, 0), (1, 0), (0, 1))
-UNROLL = 8
 TAIL = 4
 
 
@@ -88,7 +87,7 @@
     for ref in (
         ray, rby, raxh, raxl, rbxl, rbxh, rd1, rd2,
         cr_up, cr_down, cr_right, cr_left, cr_d1, cr_d2,
-        save_row_h, save_h_lo, save_h_hi, lines, sd2, cs_up, cs_down, cs_right, cs_left, cs_d1, cs_d2,
+        row_h, row_e, save_row_h, save_h_lo, save_h_hi, lines, sd2, cs_up, cs_down, cs_right, cs_left, cs_d1, cs_d2,
     ):
         ref[...] = jnp.zeros(ref.shape, f32)
 
@@ -195,7 +194,7 @@
     lanes = lax.broadcasted_iota(jnp.int32, (half, depth_z), 1)
     z_last, z_first = lanes == depth_z - 1, lanes == 0
 
-    def curl(x, part, here, beside, line, memory, forward):
+    def curl(x, part, here, beside, line, memory, forward, extra):
         turn_y = half - 1 if forward else 1
         turn_z = depth_z - 1 if forward else 1
         edge_y = is_top if forward else is_bottom
@@ -210,60 +209,77 @@
             else:
                 other = jnp.where(edge_z, 0.0, pltpu.roll(value, turn_z, 1))
             slope = other - value if forward else value - other
-            carried = keep[axis, x, part] * memory[number, x, part] + take[axis, x, part] * slope
+            before = memory[number, x, part]
+            if number in extra:
+                before = before + extra[number]
+            carried = keep[axis, x, part] * before + take[axis, x, part] * slope
             memory[number, x, part] = carried
             terms.append(slope + carried)
         return (terms[0] - terms[1], terms[2] - terms[3], terms[4] - terms[5])
 
-    blocks = depth_x // UNROLL
     no_line = [0.0, None, 0.0]
 
     def update_h(upper):
         part = high if upper else low
 
-        def run(block, _):
-            for inner in range(UNROLL):
-                x = block * UNROLL + inner
-                here = [ef[c, x, part] for c in range(3)]
-                beside = [None, ef[1, x + 1, part], ef[2, x + 1, part]]
-                line = no_line
-                if not upper:
-                    line = [ef[0, x, half:half + 1, :], None, ef[2, x, half:half + 1, :]]
-                rotation = curl(x, part, here, beside, line, me, True)
-                fresh = [hf[c, x + 1, part] - courant * rotation[c] for c in range(3)]
-                for c in range(3):
-                    hf[c, x + 1, part] = fresh[c]
-                z_copy[x, part] = here[2]
-                if upper:
-                    say[0, pl.ds(x, 1), :] = fresh[0][half - 1:half, :]
-                    say[1, pl.ds(x, 1), :] = fresh[2][half - 1:half, :]
-            return 0
-
-        lax.fori_loop(0, blocks, run, 0)
+        def fields(x):
+            if upper or x == depth_x:
+                return [ef[c, x, part] for c in range(3)]
+            scale = edge_e[x]
+            values = [
+                ef[0, x, part] - scale * row_h[1, x:x + 1, :], ef[1, x, part],
+                ef[2, x, part] + scale * row_h[0, x:x + 1, :]]
+            ef[0, x, part] = values[0]
+            ef[2, x, part] = values[2]
+            return values
+
+        here = fields(0)
+        for x in range(depth_x):
+            beside = fields(x + 1)
+            line = no_line
+            extra = {}
+            if upper:
+                amount = edge_ht[x]
+                extra = {0: amount * row_e[1, x:x + 1, :], 5: amount * row_e[0, x:x + 1, :]}
+            else:
+                line = [ef[0, x, half:half + 1, :], None, ef[2, x, half:half + 1, :]]
+            rotation = curl(x, part, here, beside, line, me, True, extra)
+            fresh = [hf[c, x + 1, part] - courant * rotation[c] for c in range(3)]
+            for c in range(3):
+                hf[c, x + 1, part] = fresh[c]
+            z_copy[x, part] = here[2]
+            if upper:
+                say[0, x:x + 1, :] = fresh[0][half - 1:half, :]
+                say[1, x:x + 1, :] = fresh[2][half - 1:half, :]
+            here = beside
 
     def update_e(upper):
         part = high if upper else low
-
-        def run(block, _):
-            for inner in range(UNROLL):
-                x = block * UNROLL + inner
-                here = [hf[c, x + 1, part] for c in range(3)]
-                beside = [None, hf[1, x, part], hf[2, x, part]]
-                line = no_line
-                if upper:
-                    line = [hf[0, x + 1, half - 1:half, :], None, hf[2, x + 1, half - 1:half, :]]
-                rotation = curl(x, part, here, beside, line, mh, False)
-                ratio = factor[x, part]
-                fresh = [ef[c, x, part] + ratio * rotation[c] for c in range(3)]
-                fresh[2] = fresh[2] - source[x, part]
-                for c in range(3):
-                    ef[c, x, part] = fresh[c]
-                if not upper:
-                    sby[0, pl.ds(x, 1), :] = fresh[0][0:1, :]
-                    sby[1, pl.ds(x, 1), :] = fresh[2][0:1, :]
-            return 0
-
-        lax.fori_loop(0, blocks, run, 0)
+        beside = [hf[c, 0, part] for c in range(3)]
+        for x in range(depth_x):
+            here = [hf[c, x + 1, part] for c in range(3)]
+            line = no_line
+            extra = {}
+            if upper:
+                scale = edge_h[x]
+                here[0] = here[0] - scale * row_e[1, x:x + 1, :]
+                here[2] = here[2] + scale * row_e[0, x:x + 1, :]
+                hf[0, x + 1, part] = here[0]
+                hf[2, x + 1, part] = here[2]
+                line = [hf[0, x + 1, half - 1:half, :], None, hf[2, x + 1, half - 1:half, :]]
+            else:
+                amount = edge_et[x]
+                extra = {0: -amount * row_h[1, x:x + 1, :], 5: -amount * row_h[0, x:x + 1, :]}
+            rotation = curl(x, part, here, beside, line, mh, False, extra)
+            ratio = factor[x, part]
+            fresh = [ef[c, x, part] + ratio * rotation[c] for c in range(3)]
+            fresh[2] = fresh[2] - source[x, part]
+            for c in range(3):
+                ef[c, x, part] = fresh[c]
+            if not upper:
+                sby[0, x:x + 1, :] = fresh[0][0:1, :]
+                sby[1, x:x + 1, :] = fresh[2][0:1, :]
+            beside = here
 
     def fix_h_side(part, side_y, side_z):
         scale = cs_right[part]
@@ -299,19 +315,10 @@
         side_z = raxl[slot, 1] - scale * save_e_lo[0]
         lines[hx_corner] = rd1[slot, 0:1, :] - cr_d1[0:1, :] * lines[ez_edge]
         fix_e_side(low, side_y, side_z)
-        for x in range(depth_x):
-            line_hx, line_hz = row_h[0, x:x + 1, :], row_h[1, x:x + 1, :]
-            amount, scale = edge_et[x], edge_e[x]
-            ef[0, x, low] = ef[0, x, low] - scale * line_hz
-            ef[2, x, low] = ef[2, x, low] + scale * line_hx
-            mh[0, x, low] = mh[0, x, low] - amount * line_hz
-            mh[5, x, low] = mh[5, x, low] - amount * line_hx
         scale = cs_down[rows_x]
         save_row_e[0] = sby[0] - scale * row_h[1]
         save_row_e[1] = sby[1] + scale * row_h[0]
         save_row_e[1, 0:1, :] = save_row_e[1, 0:1, :] - cs_down[depth_x:depth_x + 1, :] * side_y[0:1, :]
-        save_e_lo[0] = ef[1, 0, low]
-        save_e_lo[1] = ef[2, 0, low]
 
     def settle_h_low(step, first):
         arrived(step, "bxl")
@@ -347,20 +354,11 @@
             side_z = side_z - scale * save_h_hi[0]
             lines[ex_corner] = rd2[slot, 1:2, :] - cr_d2[0:1, :] * lines[hz_edge]
         fix_h_side(high, side_y, side_z)
-        for x in range(depth_x):
-            line_ex, line_ez = row_e[0, x:x + 1, :], row_e[1, x:x + 1, :]
-            amount, scale = edge_ht[x], edge_h[x]
-            hf[0, x + 1, high] = hf[0, x + 1, high] - scale * line_ez
-            hf[2, x + 1, high] = hf[2, x + 1, high] + scale * line_ex
-            me[0, x, high] = me[0, x, high] + amount * line_ez
-            me[5, x, high] = me[5, x, high] + amount * line_ex
         scale = cs_up[rows_x]
         save_row_h[0] = say[0] - scale * row_e[1]
         save_row_h[1] = say[1] + scale * row_e[0]
         save_row_h[1, last_x:depth_x, :] = (
             save_row_h[1, last_x:depth_x, :] - cs_up[depth_x:depth_x + 1, :] * side_y[half - 1:half, :])
-        save_h_hi[0] = hf[1, depth_x, high]
-        save_h_hi[1] = hf[2, depth_x, high]
 
     def settle_e_high(step):
         arrived(step, "axh")
@@ -377,18 +375,16 @@
 
     def inject(step):
         top, rest = split_two(courant * current[pl.ds(step, 1), :])
-        total = None
-        for part in (top, rest):
-            piece = jnp.dot(
-                cell_t[...] * part, depth[...], preferred_element_type=jnp.float32
-            )
-            total = piece if total is None else total + piece
+        both = jnp.concatenate([cell_t[...] * top, cell_t[...] * rest], axis=0)
+        total = jnp.dot(both, depth[...], preferred_element_type=f32)
+        total = total[:depth_x * depth_y] + total[depth_x * depth_y:]
         source[...] = total.reshape(source.shape)
 
     def read_out(values, step):
-        top, rest = split_two(values.reshape(depth_x * depth_y, depth_z))
-        picked = jnp.dot(top, depth_t[...], preferred_element_type=jnp.float32)
-        picked = picked + jnp.dot(rest, depth_t[...], preferred_element_type=jnp.float32)
+        count = depth_x * depth_y
+        both = jnp.concatenate(split_two(values.reshape(count, depth_z)), axis=0)
+        picked = jnp.dot(both, depth_t[...], preferred_element_type=f32)
+        picked = picked[:count] + picked[count:]
         chosen = jnp.sum(picked * cell_f[...], axis=0, keepdims=True)
         record[pl.ds(step, 1), :] = chosen * current[pl.ds(step, 1), :]
 
@@ -414,13 +410,11 @@
         copy.wait()
 
     def port_sums():
-        total = None
-        for part in split_two(record[...]):
-            piece = lax.dot_general(
-                part, member[...], (((1,), (1,)), ((), ())), preferred_element_type=f32
-            )
-            total = piece if total is None else total + piece
-        return total
+        both = jnp.concatenate(split_two(record[...]), axis=0)
+        total = lax.dot_general(
+            both, member[...], (((1,), (1,)), ((), ())), preferred_element_type=f32
+        )
+        return total[:steps, :] + total[steps:, :]
 
     chunk = steps // count_y
     mine = pl.ds(iy * chunk, chunk)
@@ -483,6 +477,8 @@
         inject(step - 1)
         pl.when(step > 1)(lambda: settle_e_low(step - 1))
         update_h(False)
+        save_e_lo[0] = ef[1, 0, low]
+        save_e_lo[1] = ef[2, 0, low]
         for c in (1, 2):
             saxl[c - 1] = hf[c, depth_x, low]
         send(step, "axl")
@@ -503,6 +499,8 @@
         pl.when(step == 1)(lambda: settle_h_high(step - 1, True))
         pl.when(step > 1)(lambda: settle_h_high(step - 1, False))
         update_e(True)
+        save_h_hi[0] = hf[1, depth_x, high]
+        save_h_hi[1] = hf[2, depth_x, high]
         for c in (1, 2):
             sbxh[c - 1] = ef[c, 0, high]
         pl.when(more)(lambda: send(step, "bxh"))
@@ -519,6 +517,10 @@
 
     lax.fori_loop(1, steps + 1, turn, 0)
     settle_e_low(steps)
+    for x in range(depth_x):
+        scale = edge_e[x]
+        ef[0, x, low] = ef[0, x, low] - scale * row_h[1, x:x + 1, :]
+        ef[2, x, low] = ef[2, x, low] + scale * row_h[0, x:x + 1, :]
     read_out(ef[2, pl.ds(0, depth_x)], steps - 1)
     late[...] = port_sums()[steps - TAIL:, :]
     lates = (send_late, recv_late)

time: 63.6 us -> 62.8 us (0.987)
  Pallas kernels: 62 us -> 61.2 us
    pallas_call x1, Pallas kernels: 60.9 us -> 60 us  [local(): pl.pallas_call(kernel, out_shape=(pltpu.VMEM((3, depth_x + 1, depth_y, de...]
where the time goes in v4:
time: 62.8 us; the launch traced here: 62.5 us
  Pallas kernels  61.2 us (97%)
  between operations  1.29 us (2%)
    pallas_call x1, Pallas kernels, local(): pl.pallas_call(kernel, out_shape=(pltpu.VMEM((3, depth_x + 1, depth_y, de...  60 us

profile of v4, /device:TPU:0, one launch (start us, length us, event | category | flops | bytes accessed | tf_op | source)
XLA Modules:
  0.0 62.5 jit_solution(16362072971759433223)
XLA Ops:
  1.3 60.0 %shard_map.130 = (f32[3,17,16,256]{3,2,1,0:T(8,128)S(1)}, f32[3,17,16,256]{3,2,1,0:T(8,128)S(1)}, f32[16,512]{1,0:T(8,128)S(1)}) custom-call(f32[3,16,16,256]{3,2,1,0:T(8,128)} %e_in.1, f32[3,16,16,256]{3,2,1,0:T(8,128)} %h_in.1, f32[6,16,16,256]{3,2,1,0:T(8,128)} %me_in.1, f32[6,16,16,256]{3,2,1,0:T(8,128)} %mh_in.1, s32[3,16,16,256]{3,2,1,0:T(8,128)} %grades_ref.1, ...), custom_call_target="tpu_custom_call" | custom-call | tf_op jit(solution)/shard_map/pallas_call | solution.py:582
  61.3 1.2 %shard_map.131 = (f32[3,16,16,256]{3,2,1,0:T(8,128)}, f32[3,16,16,256]{3,2,1,0:T(8,128)}, f32[16,512]{1,0:T(8,128)}) custom-call(f32[3,17,16,256]{3,2,1,0:T(8,128)S(1)} %get-tuple-element.6.ef, f32[3,17,16,256]{3,2,1,0:T(8,128)S(1)} %get-tuple-element.7.hf, f32[16,512]{1,0:T(8,128)S(1)} %get-tuple-element.8.power_ref), custom_call_target="tpu_custom_call" | custom-call | tf_op jit(solution)/shard_map/pallas_call | solution.py:635

commit v5 on v4

--- a/solution.py
+++ b/solution.py
@@ -473,7 +473,7 @@
             saxh[c - 1] = hf[c, depth_x, high]
         sd1[0:1, :] = say[0, 0:1, :]
         sd1[1:2, :] = ef[1, 0, last_y:depth_y, :]
-        send(step, "d1", "ay", "axh")
+        send(step, "d1", "axh", "ay")
         inject(step - 1)
         pl.when(step > 1)(lambda: settle_e_low(step - 1))
         update_h(False)
@@ -490,7 +490,7 @@
         for c in (1, 2):
             sbxl[c - 1] = ef[c, 0, low]
         sd2[1:2, :] = sby[0, last_x:depth_x, :]
-        pl.when(more)(lambda: send(step, "d2", "by", "bxl"))
+        pl.when(more)(lambda: send(step, "d2", "bxl", "by"))
         read_out(z_copy[...], lax.rem(step + steps - 2, steps))
         pl.when(step == steps - TAIL + 1)(reduce_one)
         pl.when(step == steps - TAIL + 3)(reduce_two)
@@ -540,11 +540,12 @@
 
 def store_kernel(ef, hf, power_ref, e_out, h_out, power_out, sem):
     depth_x = e_out.shape[1]
-    copies = [
-        pltpu.make_async_copy(ef.at[:, pl.ds(0, depth_x)], e_out, sem.at[0]),
-        pltpu.make_async_copy(hf.at[:, pl.ds(1, depth_x)], h_out, sem.at[1]),
-        pltpu.make_async_copy(power_ref, power_out, sem.at[2]),
-    ]
+    copies = [pltpu.make_async_copy(power_ref, power_out, sem.at[0])]
+    for c in range(3):
+        for number, (source_ref, first, target_ref) in enumerate(((ef, 0, e_out), (hf, 1, h_out))):
+            copies.append(pltpu.make_async_copy(
+                source_ref.at[c, pl.ds(first, depth_x)], target_ref.at[c],
+                sem.at[1 + 2 * c + number]))
     for copy in copies:
         copy.start()
     for copy in copies:
@@ -641,7 +642,7 @@
         ),
         in_specs=[vmem] * 3,
         out_specs=(anywhere,) * 3,
-        scratch_shapes=[pltpu.SemaphoreType.DMA((3,))],
+        scratch_shapes=[pltpu.SemaphoreType.DMA((7,))],
         compiler_params=pltpu.CompilerParams(vmem_limit_bytes=1024 * 1024),
     )(*fields)
 

time: 62.8 us -> 62.8 us (level)
  no operation moved by 1% of the time
where the time goes in v5:
time: 62.8 us; the launch traced here: 62.5 us
  Pallas kernels  61.2 us (97%)
  between operations  1.29 us (2%)
    pallas_call x1, Pallas kernels, local(): pl.pallas_call(kernel, out_shape=(pltpu.VMEM((3, depth_x + 1, depth_y, de...  60 us

profile of v5, /device:TPU:0, one launch (start us, length us, event | category | flops | bytes accessed | tf_op | source)
XLA Modules:
  0.0 62.5 jit_solution(6515417469911061196)
XLA Ops:
  1.3 60.0 %shard_map.130 = (f32[3,17,16,256]{3,2,1,0:T(8,128)S(1)}, f32[3,17,16,256]{3,2,1,0:T(8,128)S(1)}, f32[16,512]{1,0:T(8,128)S(1)}) custom-call(f32[3,16,16,256]{3,2,1,0:T(8,128)} %e_in.1, f32[3,16,16,256]{3,2,1,0:T(8,128)} %h_in.1, f32[6,16,16,256]{3,2,1,0:T(8,128)} %me_in.1, f32[6,16,16,256]{3,2,1,0:T(8,128)} %mh_in.1, s32[3,16,16,256]{3,2,1,0:T(8,128)} %grades_ref.1, ...), custom_call_target="tpu_custom_call" | custom-call | tf_op jit(solution)/shard_map/pallas_call | solution.py:583
  61.3 1.2 %shard_map.131 = (f32[3,16,16,256]{3,2,1,0:T(8,128)}, f32[3,16,16,256]{3,2,1,0:T(8,128)}, f32[16,512]{1,0:T(8,128)}) custom-call(f32[3,17,16,256]{3,2,1,0:T(8,128)S(1)} %get-tuple-element.6.ef, f32[3,17,16,256]{3,2,1,0:T(8,128)S(1)} %get-tuple-element.7.hf, f32[16,512]{1,0:T(8,128)S(1)} %get-tuple-element.8.power_ref), custom_call_target="tpu_custom_call" | custom-call | tf_op jit(solution)/shard_map/pallas_call | solution.py:636
